TPU v7x, 128 devices: a whole 4x4x4 slice. The times are simulated.
128 devices in a mesh: grp: 8 (over z, y_lo), slab: 16 (over y_hi, x, core).
Axes of the slice: x: 4, y: 4 (y_hi: 2, y_lo: 2; y = y_hi * 2 + y_lo), z: 4, core: 2. Of those that a mesh axis runs over, the one named last changes fastest.
Arguments:
- orbitals: float32 [16, 96, 9216], P('grp', 'slab'), may hold values from -6 to 6
- occupation: int32 [16], P('grp'), may hold values from 1 to 4
- kernel_hat: float32 [192, 36864], P('slab'), may hold values from 0.02 to 1200, as said below
- pair_mask: int32 [1], replicated, may hold values from 1 to 7
Outputs:
- exchange_terms: float32 [16, 96, 9216], P('grp', 'slab')
Inputs may be any that keep to these rules, and one draw needn't show every extreme that they name: In this round group g is paired with group g XOR pair_mask. kernel_hat is positive, and unchanged when each frequency index k is replaced by (192 - k) mod 192 in all three dimensions at once.
All inputs are finite; a program needn't handle non-finite values.
Results may differ from a plain program's by a relative error of at most 0.0001.
Values sent between devices are 32-bit elements; how exact they have to be, the bound alone decides.
No kernel may reach another device: no remote copies, remote signals or barrier semaphores. Data moves between devices by JAX's collectives and lax.ppermute only.
A program may use at most 64 MiB of HBM per device.

v0:
```python
import functools
import math

import jax
import jax.numpy as jnp
import numpy as np
from jax import lax
from jax.experimental import pallas as pl
from jax.experimental.pallas import tpu as pltpu
from jax.sharding import PartitionSpec as P

G = 96
N = 192
SLABS = 16
XS = 6
KP = 6
ROWS = 112

Y_ORDER = np.array([4 * (i % 24) + i // 24 for i in range(G)])
X_ORDER = np.array([6 * (i % SLABS) + i // SLABS for i in range(G)])


WY, WI, TX, TI, LINES = 0, 640, 1664, 2048, 2432


def split(table):
    table = jnp.asarray(table, jnp.float32)
    high = table.astype(jnp.bfloat16)
    low = (table - high.astype(jnp.float32)).astype(jnp.bfloat16)
    return high, low


def np_split(table):
    bf16 = jnp.bfloat16
    high = table.astype(np.float32).astype(bf16)
    low = (table - high.astype(np.float64)).astype(np.float32).astype(bf16)
    return np.stack([high, low])


def waves(freq, cell):
    angle = (np.outer(freq, cell) % N) * (2.0 * math.pi / N)
    return np.cos(angle), np.sin(angle)


@functools.cache
def tables():
    pair_major = np.array([[12 * d + 2 * kp for d in range(SLABS)] for kp in range(KP)]).reshape(-1)
    tz = np.zeros((384, 256))
    tv = np.zeros((256, 384))
    wy = np.zeros((320, 512))
    wi = np.zeros((2, 512, 256))
    for kz2 in range(2):
        cos, sin = waves(pair_major + kz2, np.arange(G))
        re, im = 192 * kz2, 192 * kz2 + 96
        tz[re : re + 96, 0:96], tz[re : re + 96, 128:224] = cos, sin
        tz[im : im + 96, 0:96], tz[im : im + 96, 128:224] = -sin, cos
        tv[0:96, re : re + 96], tv[0:96, im : im + 96] = cos.T / N, -sin.T / N
        tv[128:224, re : re + 96], tv[128:224, im : im + 96] = sin.T / N, cos.T / N
        cos, sin = waves(Y_ORDER, np.arange(N))
        wy[64:160, 0:192], wy[64:160, 256:448] = cos, -sin
        wy[160:256, 0:192], wy[160:256, 256:448] = sin, cos
        re, im = 64 * kz2, 64 * kz2 + 96
        wi[kz2, 0:192, re : re + 96], wi[kz2, 0:192, im : im + 96] = cos.T / N, sin.T / N
        wi[kz2, 256:448, re : re + 96], wi[kz2, 256:448, im : im + 96] = -sin.T / N, cos.T / N
    cos, sin = waves(np.arange(N), X_ORDER)
    tx = np.block([[cos, sin], [-sin, cos]])
    ti = np.block([[cos.T, -sin.T], [sin.T, cos.T]]) / N
    lines = [wy[:, :256], wy[:, 256:], wi[0], wi[1], widened(tx), widened(ti[:, :N]), widened(ti[:, N:])]
    return [np_split(t) for t in (tz, np.concatenate(lines, axis=0), tv)]


def widened(table):
    return np.pad(table, ((0, 0), (0, 256 - N)))


def mm(left, right, form=(1, 0)):
    def one(a, b):
        return lax.dot_general(
            a, b, (((form[0],), (form[1],)), ((), ())), preferred_element_type=jnp.float32
        )

    return one(left[0], right[0]) + (one(left[0], right[1]) + one(left[1], right[0]))


def plane(ref, x, orbital):
    base = 144 * x + orbital
    tiles = [ref[pl.ds(base + 2 * tile, 24, stride=6), :] for tile in range(3)]
    return jnp.concatenate(tiles, axis=1)


def lines(dense):
    return jnp.concatenate([dense[:, 96 * q : 96 * q + 96] for q in range(4)], axis=0)


def dense_of(rows):
    return jnp.concatenate([rows[24 * q : 24 * q + 24] for q in range(4)], axis=1)


def near_kernel(own_hbm, tz_hbm, own_ref, tz_ref, sems):
    copies = [
        pltpu.make_async_copy(own_hbm, own_ref, sems.at[0]),
        pltpu.make_async_copy(tz_hbm, tz_ref, sems.at[1]),
    ]
    for copy in copies:
        copy.start()
    for copy in copies:
        copy.wait()


def spread_kernel(
    upper_ref, own_ref, their_ref, tz_ref, their_hbm, out_hbm, out_ref, sems, their_sem
):
    kept = pltpu.make_async_copy(their_ref, their_hbm, their_sem)
    kept.start()
    upper = upper_ref[0] == 1
    pad = jnp.zeros((G, 32), jnp.float32)
    outs = []
    for x in range(XS):
        theirs = [plane(their_ref, x, o) for o in range(2)]
        first = jnp.where(upper, theirs[1], theirs[0])
        second = jnp.where(upper, theirs[0], theirs[1])
        one = lines(plane(own_ref, x, 0) * first)
        two = lines(plane(own_ref, x, 1) * second)
        density = jnp.concatenate([one, pad, two, pad], axis=1)
        lined = mm((tz_ref[0], tz_ref[1]), split(density), (1, 1))
        wide = jnp.concatenate([lined[96 * j : 96 * j + 96] for j in range(4)], axis=1)
        for kp in range(KP):
            for tile in range(3):
                out_ref[pl.ds(18 * x + 6 * tile + kp, SLABS, stride=ROWS), :] = wide[
                    16 * kp : 16 * kp + 16, 128 * tile : 128 * tile + 128
                ]
        if x in (3, 5):
            first_row, count = (0, 72) if x == 3 else (72, 40)
            if x == 5:
                for slab in range(SLABS):
                    out_ref[ROWS * slab + 108 : ROWS * slab + 112, :] = jnp.zeros((4, 128), jnp.float32)
            for slab in range(SLABS):
                place = pl.ds(ROWS * slab + first_row, count)
                outs.append(
                    pltpu.make_async_copy(out_ref.at[place], out_hbm.at[place], sems.at[len(outs)])
                )
                outs[-1].start()
    for copy in outs:
        copy.wait()
    kept.wait()


def line_kernel(in_ref, hat_ref, table_hbm, out_ref, y_ref, u_ref, table_ref, sems):
    fetches = []
    for row, count in ((WY, WI - WY), (TX, LINES - TX), (WI, TX - WI)):
        place = (slice(None), pl.ds(row, count))
        pair = (table_hbm.at[place], table_ref.at[place])
        fetches.append(pltpu.make_async_copy(*pair, sems.at[len(fetches)]))
    for copy in fetches:
        copy.start()
    def table(row, count, columns=256):
        return [table_ref[part, row : row + count, :columns] for part in range(2)]

    pieces = []
    for kp in range(KP):
        for x in range(XS):
            pieces.append(
                jnp.concatenate(
                    [
                        in_ref[pl.ds(18 * x + 6 * tile + kp, SLABS, stride=ROWS), :]
                        for tile in range(3)
                    ],
                    axis=1,
                )
            )
    data = split(jnp.concatenate(pieces, axis=0))
    fetches[0].wait()
    for kz2 in range(2):
        window = [part[:, 128 * kz2 : 128 * kz2 + 256] for part in data]
        for c in range(2):
            result = mm(window, table(WY + 320 * c + 64 * (1 - kz2), 256))
            for kp in range(KP):
                y_ref[2 * kp + kz2, 96 * c : 96 * c + 96, :] = result[96 * kp : 96 * kp + 96]
    fetches[1].wait()
    for kz in range(2 * KP):
        lined = split(y_ref[kz, :, :N])
        spectrum = mm(table(TX, 384, N), lined)
        hat = hat_ref[kz]
        u_ref[kz, :, :N] = mm(table(TI, N, N), split(spectrum[:N] * hat)) + mm(
            table(TI + N, N, N), split(spectrum[N:] * hat)
        )
    fetches[2].wait()
    sides = []
    for kz2 in range(2):
        rows = [
            [u_ref[2 * kp + kz2, G * c : G * c + G, :N] for kp in range(KP)] for c in range(2)
        ]
        re, im = [split(jnp.concatenate(part, axis=0)) for part in rows]
        first = WI + 512 * kz2
        sides.append(mm(re, table(first, N)) + mm(im, table(first + 256, N)))
    wide = [sides[0][:, :128], sides[0][:, 128:] + sides[1][:, :128], sides[1][:, 128:]]
    for kp in range(KP):
        for x in range(XS):
            for tile in range(3):
                row = 96 * kp + 16 * x
                out_ref[pl.ds(18 * x + 6 * tile + kp, SLABS, stride=ROWS), :] = wide[tile][
                    row : row + 16
                ]


def term_kernel(
    upper_ref, occupation_ref, in_ref, own_ref, their_hbm, tv_ref, kept_ref, sent_ref, their_ref,
    field_ref, sem
):
    fetch = pltpu.make_async_copy(their_hbm, their_ref, sem)
    fetch.start()
    upper = upper_ref[0] == 1
    table = (tv_ref[0], tv_ref[1])
    weight = [0.25 * occupation_ref[o].astype(jnp.float32) for o in range(2)]
    for x in range(XS):
        pieces = [
            jnp.concatenate(
                [
                    in_ref[pl.ds(18 * x + 6 * tile + kp, SLABS, stride=ROWS), :]
                    for tile in range(3)
                ],
                axis=1,
            )
            for kp in range(KP)
        ]
        wide = jnp.concatenate(pieces, axis=0)
        stacked = jnp.concatenate([wide[:, 96 * j : 96 * j + 96] for j in range(4)], axis=0)
        fields = mm(table, split(stacked)).T
        field_ref[0, x] = dense_of(fields[:, :96])
        field_ref[1, x] = dense_of(fields[:, 128:224])
    fetch.wait()
    for x in range(XS):
        one, two = field_ref[0, x], field_ref[1, x]
        theirs = [plane(their_ref, x, o) for o in range(2)]
        first = jnp.where(upper, theirs[1], theirs[0])
        second = jnp.where(upper, theirs[0], theirs[1])
        kept = [one * first, two * second]
        mine_one = one * plane(own_ref, x, 0) * weight[0]
        mine_two = two * plane(own_ref, x, 1) * weight[1]
        sent = [jnp.where(upper, mine_two, mine_one), jnp.where(upper, mine_one, mine_two)]
        for o in range(2):
            for tile in range(3):
                place = pl.ds(144 * x + o + 2 * tile, 24, stride=6)
                kept_ref[place, :] = kept[o][:, 128 * tile : 128 * tile + 128]
                sent_ref[place, :] = sent[o][:, 128 * tile : 128 * tile + 128]
    row = lax.broadcasted_iota(jnp.int32, (8, 128), 0)
    sent_ref[864:872, :] = jnp.where(row % 2 == 1, weight[1], weight[0])


PARTS = ((864, 8), (0, 216), (216, 216), (432, 216), (648, 216))


def sum_kernel(upper_ref, kept_ref, come_hbm, out_hbm, come_ref, out_ref, sems):
    fetches, outs = [], []
    for k, (row, count) in enumerate(PARTS):
        place = pl.ds(row, count)
        fetches.append(pltpu.make_async_copy(come_hbm.at[place], come_ref.at[place], sems.at[k]))
        fetches[-1].start()
    upper = upper_ref[0] == 1
    odd_row = lax.broadcasted_iota(jnp.int32, (216, 128), 0) % 2 == 1
    fetches[0].wait()
    even = jnp.where(upper, come_ref[865:866, :], come_ref[864:865, :])
    odd = jnp.where(upper, come_ref[864:865, :], come_ref[865:866, :])
    weight = jnp.where(odd_row, odd, even)
    for k, (row, count) in enumerate(PARTS[1:], 1):
        place = pl.ds(row, count)
        fetches[k].wait()
        out_ref[place, :] = -(kept_ref[place, :] * weight + come_ref[place, :])
        outs.append(pltpu.make_async_copy(out_ref.at[place], out_hbm.at[place], sems.at[4 + k]))
        outs[-1].start()
    for copy in outs:
        copy.wait()


SMEM = pl.BlockSpec(memory_space=pltpu.SMEM)
VMEM = pl.BlockSpec(memory_space=pltpu.VMEM)
HBM = pl.BlockSpec(memory_space=pltpu.HBM)


def call(kernel, ins, outs, args, scratch=(), out_spec=VMEM, limit=28_000_000):
    shapes = [o if isinstance(o, jax.ShapeDtypeStruct) else jax.ShapeDtypeStruct(o, jnp.float32) for o in outs]
    many = len(shapes) > 1
    return pl.pallas_call(
        kernel,
        out_shape=shapes if many else shapes[0],
        in_specs=ins,
        out_specs=[out_spec] * len(outs) if many else out_spec,
        scratch_shapes=scratch,
        compiler_params=pltpu.CompilerParams(vmem_limit_bytes=limit),
    )(*args)


def to_partner(value, pair_bits, then=lambda come: come, *others):
    group_count = lax.axis_size("grp")

    def by_mask(mask):
        pairs = [(source, source ^ mask) for source in range(group_count)]
        return lambda given: then(lax.ppermute(given[0], "grp", pairs), *given[1:])

    branches = [by_mask(mask) for mask in range(1, group_count)]
    return lax.switch(pair_bits - 1, branches, (value, *others))


def to_rows(planes):
    return planes.reshape(2, XS, 72, 128).transpose(1, 2, 0, 3).reshape(864, 128)


def from_rows(rows):
    return rows.reshape(XS, 72, 2, 128).transpose(2, 0, 1, 3).reshape(2, XS, G * G)


def exchange(chunks):
    chunks = chunks.reshape(SLABS, ROWS, 128)
    moved = lax.all_to_all(chunks, "slab", split_axis=0, concat_axis=0, tiled=True)
    return moved.reshape(SLABS * ROWS, 128)


def local(orbitals, occupation, kernel_hat, pair_mask):
    tz, lines_table, tv = [jnp.asarray(t) for t in tables()]
    pair_bits = pair_mask[0]
    own_group = lax.axis_index("grp")
    upper = (own_group > jnp.bitwise_xor(own_group, pair_bits)).astype(jnp.int32).reshape(1)
    own = to_rows(orbitals)
    chunk = (SLABS * ROWS, 128)
    rows = pltpu.VMEM((864, 128), jnp.float32)

    def spread_out(theirs, own, upper, tz):
        near = [jax.ShapeDtypeStruct(a.shape, a.dtype) for a in (own, tz)]
        own, tz = call(near_kernel, [HBM] * 2, near, (own, tz), [pltpu.SemaphoreType.DMA((2,))])
        scratch = [pltpu.VMEM(chunk, jnp.float32), pltpu.SemaphoreType.DMA((2 * SLABS,))]
        scratch.append(pltpu.SemaphoreType.DMA)
        operands = (upper, own, theirs, tz)
        outs = [(864, 128), chunk]
        return call(spread_kernel, [SMEM] + [VMEM] * 3, outs, operands, scratch, HBM)

    theirs, spread = to_partner(own, pair_bits, spread_out, own, upper, tz)
    hat = kernel_hat.reshape(2 * KP, N, N).transpose(0, 2, 1)
    scratch = [pltpu.VMEM((2 * KP, N, 256), jnp.float32)] * 2
    scratch += [pltpu.VMEM(lines_table.shape, lines_table.dtype), pltpu.SemaphoreType.DMA((3,))]
    lined = call(
        line_kernel,
        [VMEM, VMEM, HBM],
        [chunk],
        (exchange(spread), hat, lines_table),
        scratch,
        limit=51_000_000,
    )
    back = exchange(lined)
    kept, sent = call(
        term_kernel,
        [SMEM, SMEM, VMEM, VMEM, HBM, VMEM],
        [(864, 128), (872, 128)],
        (upper, occupation, back, own, theirs, tv),
        [rows, pltpu.VMEM((2, XS, 24, 384), jnp.float32), pltpu.SemaphoreType.DMA],
    )

    come = to_partner(sent, pair_bits)
    scratch = [pltpu.VMEM((872, 128), jnp.float32), rows, pltpu.SemaphoreType.DMA((9,))]
    total = call(sum_kernel, [SMEM, VMEM, HBM], [(864, 128)], (upper, kept, come), scratch, HBM)
    return from_rows(total)


def solution(mesh):
    return jax.shard_map(
        local,
        mesh=mesh,
        in_specs=(P("grp", "slab", None), P("grp"), P("slab", None), P()),
        out_specs=P("grp", "slab", None),
        check_vma=False,
    )
```

profile of v0, /device:TPU:0, one launch (start us, length us, event | category | flops | bytes accessed | tf_op | source)
XLA Modules:
  0.0 85.3 jit_solution(7033709323147739029)
XLA Ops:
  0.7 0.0 copy-start.3
  0.7 17.0 %conditional.2 = ((f32[864,128]{1,0:T(8,128)}, f32[1792,128]{1,0:T(8,128)})) conditional(s32[]{:T(128)} %clamp.4, (f32[864,128]{1,0:T(8,128)}, bf16[2,384,256]{2,1,0:T(8,128)(2,1)}, s32[1]{0:T(128)}) %tuple.69, (f32[864,128]{1,0:T(8,128)}, bf16[2,384,256]{2,1,0:T(8,128)(2,1)}, s32[1]{0:T(128)}) %tuple.70, ...), branch_computations={%region_0.0_spmd, %region_1.0_spmd, %region_2.0_spmd, %region_3.0_... | conditional | bytes 1769520 | solution.py:301
  0.7 4.2 %collective-permute-start.5 = (f32[864,128]{1,0:T(8,128)}, f32[864,128]{1,0:T(8,128)S(1)}, u32[]{:S(2)}, u32[]{:S(2)}) collective-permute-start(f32[864,128]{1,0:T(8,128)} %get-tuple-element.88.own_hbm), channel_id=1, source_target_pairs={{0,96},{16,112},{32,64},{48,80},{64,32},{80,48},{96,0},{112,16},{1... | collective-permute-start | bytes 1327112 | tf_op jit(solution)/shard_map/cond/branch_5_fun/ppermute | solution.py:298
  4.9 1.1 %branch_5_fun.2 = (f32[864,128]{1,0:T(8,128)S(1)}, bf16[2,384,256]{2,1,0:T(8,128)(2,1)S(1)}) custom-call(f32[864,128]{1,0:T(8,128)} %get-tuple-element.88.own_hbm, bf16[2,384,256]{2,1,0:T(8,128)(2,1)} %get-tuple-element.89.tz_hbm), custom_call_target="tpu_custom_call" | custom-call | tf_op jit(solution)/shard_map/cond/branch_5_fun/pallas_call | solution.py:283
  6.1 9.2 %collective-permute-done.5.their_ref = f32[864,128]{1,0:T(8,128)S(1)} collective-permute-done((f32[864,128]{1,0:T(8,128)}, f32[864,128]{1,0:T(8,128)S(1)}, u32[]{:S(2)}, u32[]{:S(2)}) %collective-permute-start.5) | collective-permute-done | bytes 442400 | tf_op jit(solution)/shard_map/cond/branch_5_fun/ppermute | solution.py:298
  15.3 2.4 %branch_5_fun.3 = (f32[864,128]{1,0:T(8,128)}, f32[1792,128]{1,0:T(8,128)}) custom-call(s32[1]{0:T(128)} %get-tuple-element.87.upper_ref, f32[864,128]{1,0:T(8,128)S(1)} %get-tuple-element.90.own_ref, f32[864,128]{1,0:T(8,128)S(1)} %collective-permute-done.5.their_ref, bf16[2,384,256]{2,1,0:T(8,128)(2,1)S(1)} %get-tuple-element.91.tz_ref), custom_call_target="tpu_custom_call" | custom-call | tf_op jit(solution)/shard_map/cond/branch_5_fun/pallas_call | solution.py:283
  17.7 7.1 %all-to-all-start = ((f32[16,112,128]{2,1,0:T(8,128)}), f32[16,112,128]{2,1,0:T(8,128)S(1)}, u32[]{:S(2)}, u32[]{:S(2)}) async-start(f32[16,112,128]{2,1,0:T(8,128)} %bitcast.5), calls=%async_computation | async-start | bytes 1835008 | tf_op jit(solution)/shard_map/all_to_all | solution.py:314
  24.8 0.0 copy-done.3
  24.8 2.2 %reshape.38 = f32[12,192,192]{2,1,0:T(8,128)} reshape(f32[12,36864]{1,0:T(8,128)S(1)} %copy-done.3) | data formatting | bytes 3538944 | tf_op jit(solution)/shard_map/reshape | solution.py:337
  26.9 2.2 %copy.11 = f32[12,192,192]{1,2,0:T(8,128)S(1)} copy(f32[12,192,192]{2,1,0:T(8,128)} %reshape.38) | data formatting | bytes 3538944 | tf_op jit(solution)/shard_map/reshape | solution.py:337
  29.1 12.2 %all-to-all-done = f32[16,112,128]{2,1,0:T(8,128)S(1)} async-done(((f32[16,112,128]{2,1,0:T(8,128)}), f32[16,112,128]{2,1,0:T(8,128)S(1)}, u32[]{:S(2)}, u32[]{:S(2)}) %all-to-all-start) | async-done | bytes 917536 | tf_op jit(solution)/shard_map/all_to_all | solution.py:314
  41.3 0.0 copy-start
  41.3 0.0 copy-start.1
  41.3 0.0 copy-start.2
  41.3 0.0 copy-start.4
  41.3 7.7 %shard_map.73 = f32[1792,128]{1,0:T(8,128)S(1)} custom-call(f32[1792,128]{1,0:T(8,128)S(1)} %bitcast.20, f32[12,192,192]{2,1,0:T(8,128)S(1)} %bitcast.19, bf16[2,2432,256]{2,1,0:T(8,128)(2,1)} %constant.20.clone.table_hbm), custom_call_target="tpu_custom_call" | custom-call | tf_op jit(solution)/shard_map/pallas_call | solution.py:283
  49.0 18.9 %all_to_all.10 = f32[16,112,128]{2,1,0:T(8,128)S(1)} all-to-all(f32[16,112,128]{2,1,0:T(8,128)S(1)} %bitcast.21), channel_id=1, replica_groups=mesh['grp'=8,'slab'=16] {'slab'}, dimensions={0} | all-to-all | bytes 1835008 | tf_op jit(solution)/shard_map/all_to_all | solution.py:314
  67.9 0.0 copy-done
  67.9 0.0 copy-done.1
  67.9 0.0 copy-done.2
  67.9 0.0 copy-done.4
  67.9 2.4 %shard_map.74 = (f32[864,128]{1,0:T(8,128)S(1)}, f32[872,128]{1,0:T(8,128)S(1)}) custom-call(s32[1]{0:T(128)} %bitcast.1.upper_ref, s32[2]{0:T(128)S(1)} %copy-done.1, f32[1792,128]{1,0:T(8,128)S(1)} %bitcast.22, f32[864,128]{1,0:T(8,128)S(1)} %bitcast.30, f32[864,128]{1,0:T(8,128)S(1)} %copy-done.4, bf16[2,256,384]{2,1,0:T(8,128)(2,1)S(1)} %copy-done), custom_call_target="tpu_custom_call" | custom-call | tf_op jit(solution)/shard_map/pallas_call | solution.py:283
  70.3 13.0 %conditional.3 = (f32[872,128]{1,0:T(8,128)}) conditional(s32[]{:T(128)} %clamp.4, f32[872,128]{1,0:T(8,128)S(1)} %get-tuple-element.104, f32[872,128]{1,0:T(8,128)S(1)} %get-tuple-element.104, f32[872,128]{1,0:T(8,128)S(1)} %get-tuple-element.104, f32[872,128]{1,0:T(8,128)S(1)} %get-tuple-element.104, ...), branch_computations={%region_7.0_spmd, %region_8.0_spmd, %region_9.0_spmd, %region_10.0... | conditional | bytes 1785904 | solution.py:301
  70.3 3.0 %collective-permute-start.12 = (f32[872,128]{1,0:T(8,128)S(1)}, f32[872,128]{1,0:T(8,128)}, u32[]{:S(2)}, u32[]{:S(2)}) collective-permute-start(f32[872,128]{1,0:T(8,128)S(1)} %param.12), channel_id=1, source_target_pairs={{0,96},{16,112},{32,64},{48,80},{64,32},{80,48},{96,0},{112,16},{1... | collective-permute-start | bytes 1339400 | tf_op jit(solution)/shard_map/cond/branch_5_fun/ppermute | solution.py:298
  73.4 10.0 %collective-permute-done.12 = f32[872,128]{1,0:T(8,128)} collective-permute-done((f32[872,128]{1,0:T(8,128)S(1)}, f32[872,128]{1,0:T(8,128)}, u32[]{:S(2)}, u32[]{:S(2)}) %collective-permute-start.12) | collective-permute-done | bytes 446496 | tf_op jit(solution)/shard_map/cond/branch_5_fun/ppermute | solution.py:298
  83.3 1.8 %shard_map.75 = f32[864,128]{1,0:T(8,128)} custom-call(s32[1]{0:T(128)} %bitcast.1.upper_ref, f32[864,128]{1,0:T(8,128)S(1)} %get-tuple-element.103.kept_ref, f32[872,128]{1,0:T(8,128)} %get-tuple-element.120.come_hbm), custom_call_target="tpu_custom_call" | custom-call | tf_op jit(solution)/shard_map/pallas_call | solution.py:283
Async XLA Ops:
  0.7 24.1 %copy-start.3 = (f32[12,36864]{1,0:T(8,128)S(1)}, f32[12,36864]{1,0:T(8,128)}, u32[]{:S(2)}) copy-start(f32[12,36864]{1,0:T(8,128)} %param.23) | copy-start | bytes 5308420
  0.7 14.6 %collective-permute-start.5 = (f32[864,128]{1,0:T(8,128)}, f32[864,128]{1,0:T(8,128)S(1)}, u32[]{:S(2)}, u32[]{:S(2)}) collective-permute-start(f32[864,128]{1,0:T(8,128)} %get-tuple-element.88.own_hbm), channel_id=1, source_target_pairs={{0,96},{16,112},{32,64},{48,80},{64,32},{80,48},{96,0},{112,16},{1... | collective-permute-start | bytes 1327112 | tf_op jit(solution)/shard_map/cond/branch_5_fun/ppermute | solution.py:298
  17.7 23.6 %all-to-all-start = ((f32[16,112,128]{2,1,0:T(8,128)}), f32[16,112,128]{2,1,0:T(8,128)S(1)}, u32[]{:S(2)}, u32[]{:S(2)}) async-start(f32[16,112,128]{2,1,0:T(8,128)} %bitcast.5), calls=%async_computation | async-start | bytes 1835008 | tf_op jit(solution)/shard_map/all_to_all | solution.py:314
  41.3 26.6 %copy-start = (bf16[2,256,384]{2,1,0:T(8,128)(2,1)S(1)}, bf16[2,256,384]{2,1,0:T(8,128)(2,1)}, u32[]{:S(2)}) copy-start(bf16[2,256,384]{2,1,0:T(8,128)(2,1)} %constant.21.clone.tv_ref) | copy-start | bytes 1179652
  41.3 26.6 %copy-start.1 = (s32[2]{0:T(128)S(1)}, s32[2]{0:T(128)}, u32[]{:S(2)}) copy-start(s32[2]{0:T(128)} %occupation_ref.1) | copy-start | bytes 28
  41.3 26.6 %copy-start.2 = (f32[2,6,9216]{2,0,1:T(2,128)S(1)}, f32[2,6,9216]{2,0,1:T(2,128)}, u32[]{:S(2)}) copy-start(f32[2,6,9216]{2,0,1:T(2,128)} %param.21) | copy-start | bytes 1327108
  41.3 26.6 %copy-start.4 = (f32[864,128]{1,0:T(8,128)S(1)}, f32[864,128]{1,0:T(8,128)}, u32[]{:S(2)}) copy-start(f32[864,128]{1,0:T(8,128)} %get-tuple-element.102.their_hbm) | copy-start | bytes 1327108
  70.3 13.0 %collective-permute-start.12 = (f32[872,128]{1,0:T(8,128)S(1)}, f32[872,128]{1,0:T(8,128)}, u32[]{:S(2)}, u32[]{:S(2)}) collective-permute-start(f32[872,128]{1,0:T(8,128)S(1)} %param.12), channel_id=1, source_target_pairs={{0,96},{16,112},{32,64},{48,80},{64,32},{80,48},{96,0},{112,16},{1... | collective-permute-start | bytes 1339400 | tf_op jit(solution)/shard_map/cond/branch_5_fun/ppermute | solution.py:298
where the time goes:
time: 85.7 us; the launch traced here: 85.3 us
  waiting for transfers between devices  31.4 us (37%)
  blocking collectives  18.9 us (22%)
  Pallas kernels  15.4 us (18%)
  starting transfers between devices  14.3 us (17%)
  local copies, waits for them, and re-layouts  4.38 us (5%)
  between operations  0.89 us (1%)
    ppermute x2, waiting for transfers between devices, by_mask(): return lambda given: then(lax.ppermute(given[0], 'grp', pairs), *given[1:])  19.2 us
    all_to_all x1, blocking collectives, exchange(): lax.all_to_all(chunks, 'slab', split_axis=0, concat_axis=0, tiled=True)  18.9 us
    pallas_call x5, Pallas kernels, call(): pl.pallas_call(kernel, out_shape=shapes if many else shapes[0], in_specs=...  15.4 us
    all_to_all x1, waiting for transfers between devices, exchange(): lax.all_to_all(chunks, 'slab', split_axis=0, concat_axis=0, tiled=True)  12.2 us
    ppermute x2, starting transfers between devices, by_mask(): return lambda given: then(lax.ppermute(given[0], 'grp', pairs), *given[1:])  7.26 us
    all_to_all x1, starting transfers between devices, exchange(): lax.all_to_all(chunks, 'slab', split_axis=0, concat_axis=0, tiled=True)  7.05 us
    reshape x2, local copies, waits for them, and re-layouts, local(): hat = kernel_hat.reshape(2 * KP, N, N).transpose(0, 2, 1)  4.36 us
  transfers between devices with their start and end apart: 3, of which 3 were waited for; matrix products, arithmetic and copies ran while one was open for 5% of the time, Pallas kernels for 1%

commit v1 on v0

--- a/solution.py
+++ b/solution.py
@@ -20,7 +20,7 @@
 X_ORDER = np.array([6 * (i % SLABS) + i // SLABS for i in range(G)])
 
 
-WY, WI, TX, TI, LINES = 0, 640, 1664, 2048, 2432
+WY, WI, TX, TI, LINES = 0, 640, 1280, 1472, 1664
 
 
 def split(table):
@@ -47,8 +47,8 @@
     pair_major = np.array([[12 * d + 2 * kp for d in range(SLABS)] for kp in range(KP)]).reshape(-1)
     tz = np.zeros((384, 256))
     tv = np.zeros((256, 384))
-    wy = np.zeros((320, 512))
-    wi = np.zeros((2, 512, 256))
+    wy = np.zeros((640, 256))
+    wi = np.zeros((640, 256))
     for kz2 in range(2):
         cos, sin = waves(pair_major + kz2, np.arange(G))
         re, im = 192 * kz2, 192 * kz2 + 96
@@ -56,21 +56,21 @@
         tz[im : im + 96, 0:96], tz[im : im + 96, 128:224] = -sin, cos
         tv[0:96, re : re + 96], tv[0:96, im : im + 96] = cos.T / N, -sin.T / N
         tv[128:224, re : re + 96], tv[128:224, im : im + 96] = sin.T / N, cos.T / N
-        cos, sin = waves(Y_ORDER, np.arange(N))
-        wy[64:160, 0:192], wy[64:160, 256:448] = cos, -sin
-        wy[160:256, 0:192], wy[160:256, 256:448] = sin, cos
-        re, im = 64 * kz2, 64 * kz2 + 96
-        wi[kz2, 0:192, re : re + 96], wi[kz2, 0:192, im : im + 96] = cos.T / N, sin.T / N
-        wi[kz2, 256:448, re : re + 96], wi[kz2, 256:448, im : im + 96] = -sin.T / N, cos.T / N
-    cos, sin = waves(np.arange(N), X_ORDER)
-    tx = np.block([[cos, sin], [-sin, cos]])
-    ti = np.block([[cos.T, -sin.T], [sin.T, cos.T]]) / N
-    lines = [wy[:, :256], wy[:, 256:], wi[0], wi[1], widened(tx), widened(ti[:, :N]), widened(ti[:, N:])]
+    cos, sin = waves(Y_ORDER, np.arange(N))
+    wy[64:160, :N], wy[160:256, :N] = cos, sin
+    wy[384:480, :N], wy[480:576, :N] = -sin, cos
+    wi[64:256, 0:96], wi[64:256, 96:192] = cos.T / N, sin.T / N
+    wi[384:576, 0:96], wi[384:576, 96:192] = -sin.T / N, cos.T / N
+    cos, sin = waves(np.arange(G), X_ORDER)
+    sin[0] = waves(np.array([G]), X_ORDER)[0][0]
+    tx = np.concatenate([cos, sin], axis=0)
+    ti = np.block([[cos.T, -sin.T], [cos.T, sin.T]]) / N
+    lines = [wy, wi, widened(tx), widened(ti)]
     return [np_split(t) for t in (tz, np.concatenate(lines, axis=0), tv)]
 
 
 def widened(table):
-    return np.pad(table, ((0, 0), (0, 256 - N)))
+    return np.pad(table, ((0, 0), (0, 256 - table.shape[1])))
 
 
 def mm(left, right, form=(1, 0)):
@@ -145,12 +145,20 @@
     kept.wait()
 
 
-def line_kernel(in_ref, hat_ref, table_hbm, out_ref, y_ref, u_ref, table_ref, sems):
+def side_by_side(left, right):
+    right = pltpu.roll(right, 64, 1)
+    return jnp.concatenate(
+        [left[:, :128], left[:, 128:] + right[:, :128], right[:, 128:]], axis=1
+    )
+
+
+def line_kernel(in_ref, hat_hbm, table_hbm, out_ref, y_ref, u_ref, hat_ref, table_ref, sems):
     fetches = []
     for row, count in ((WY, WI - WY), (TX, LINES - TX), (WI, TX - WI)):
         place = (slice(None), pl.ds(row, count))
         pair = (table_hbm.at[place], table_ref.at[place])
         fetches.append(pltpu.make_async_copy(*pair, sems.at[len(fetches)]))
+    fetches.insert(2, pltpu.make_async_copy(hat_hbm, hat_ref, sems.at[3]))
     for copy in fetches:
         copy.start()
     def table(row, count, columns=256):
@@ -170,36 +178,49 @@
             )
     data = split(jnp.concatenate(pieces, axis=0))
     fetches[0].wait()
-    for kz2 in range(2):
-        window = [part[:, 128 * kz2 : 128 * kz2 + 256] for part in data]
-        for c in range(2):
-            result = mm(window, table(WY + 320 * c + 64 * (1 - kz2), 256))
-            for kp in range(KP):
-                y_ref[2 * kp + kz2, 96 * c : 96 * c + 96, :] = result[96 * kp : 96 * kp + 96]
+    for c in range(2):
+        result = []
+        for kz2 in range(2):
+            window = [part[:, 128 * kz2 : 128 * kz2 + 256] for part in data]
+            result.append(mm(window, table(WY + 320 * c + 64 * (1 - kz2), 256)))
+        paired = side_by_side(*result)
+        for kp in range(KP):
+            lanes = slice(384 * (kp % 2), 384 * (kp % 2) + 384)
+            y_ref[kp // 2, c, :, lanes] = paired[96 * kp : 96 * kp + 96]
     fetches[1].wait()
-    for kz in range(2 * KP):
-        lined = split(y_ref[kz, :, :N])
-        spectrum = mm(table(TX, 384, N), lined)
-        hat = hat_ref[kz]
-        u_ref[kz, :, :N] = mm(table(TI, N, N), split(spectrum[:N] * hat)) + mm(
-            table(TI + N, N, N), split(spectrum[N:] * hat)
-        )
     fetches[2].wait()
+    first_row = lax.broadcasted_iota(jnp.int32, (G, 768), 0) == 0
+    for q in range(3):
+        forward = table(TX, N, G)
+        re = mm(forward, split(y_ref[q, 0]))
+        im = mm(forward, split(y_ref[q, 1]))
+        even, odd = hat_ref[q, :G], hat_ref[q, G:N]
+        even_sin = jnp.where(first_row, hat_ref[q, N : N + 1], even)
+        cos_re = even * re[:G] + odd * im[G:]
+        sin_im = odd * im[:G] - even_sin * re[G:]
+        cos_im = even * im[:G] - odd * re[G:]
+        sin_re = odd * re[:G] + even_sin * im[G:]
+        u_ref[q, 0] = mm(table(TI, G, N), split(jnp.concatenate([cos_re, sin_im], axis=0)))
+        u_ref[q, 1] = mm(table(TI + G, G, N), split(jnp.concatenate([cos_im, sin_re], axis=0)))
+    fetches[3].wait()
     sides = []
     for kz2 in range(2):
-        rows = [
-            [u_ref[2 * kp + kz2, G * c : G * c + G, :N] for kp in range(KP)] for c in range(2)
-        ]
-        re, im = [split(jnp.concatenate(part, axis=0)) for part in rows]
-        first = WI + 512 * kz2
-        sides.append(mm(re, table(first, N)) + mm(im, table(first + 256, N)))
-    wide = [sides[0][:, :128], sides[0][:, 128:] + sides[1][:, :128], sides[1][:, 128:]]
+        parts = []
+        for c in range(2):
+            rows = []
+            for kp in range(KP):
+                lane = 384 * (kp % 2) + 128 * kz2
+                rows.append(u_ref[kp // 2, c, :, lane : lane + 256])
+            back = split(jnp.concatenate(rows, axis=0))
+            parts.append(mm(back, table(WI + 320 * c + 64 * (1 - kz2), 256)))
+        sides.append(parts[0] + parts[1])
+    wide = side_by_side(*sides)
     for kp in range(KP):
         for x in range(XS):
             for tile in range(3):
                 row = 96 * kp + 16 * x
-                out_ref[pl.ds(18 * x + 6 * tile + kp, SLABS, stride=ROWS), :] = wide[tile][
-                    row : row + 16
+                out_ref[pl.ds(18 * x + 6 * tile + kp, SLABS, stride=ROWS), :] = wide[
+                    row : row + 16, 128 * tile : 128 * tile + 128
                 ]
 
 
@@ -315,6 +336,15 @@
     return moved.reshape(SLABS * ROWS, 128)
 
 
+def fold_table():
+    table = np.zeros((200, N), np.float32)
+    for k in range(1, G):
+        table[k, k] = table[k, N - k] = 1.0
+        table[G + k, k], table[G + k, N - k] = 1.0, -1.0
+    table[0, 0] = table[N, G] = 1.0
+    return table
+
+
 def local(orbitals, occupation, kernel_hat, pair_mask):
     tz, lines_table, tv = [jnp.asarray(t) for t in tables()]
     pair_bits = pair_mask[0]
@@ -334,16 +364,22 @@
         return call(spread_kernel, [SMEM] + [VMEM] * 3, outs, operands, scratch, HBM)
 
     theirs, spread = to_partner(own, pair_bits, spread_out, own, upper, tz)
-    hat = kernel_hat.reshape(2 * KP, N, N).transpose(0, 2, 1)
-    scratch = [pltpu.VMEM((2 * KP, N, 256), jnp.float32)] * 2
-    scratch += [pltpu.VMEM(lines_table.shape, lines_table.dtype), pltpu.SemaphoreType.DMA((3,))]
+    hat = jnp.einsum(
+        "rx,qnx->qrn",
+        jnp.asarray(fold_table()),
+        kernel_hat.reshape(3, 4 * N, N),
+        precision=lax.Precision.HIGHEST,
+    )
+    scratch = [pltpu.VMEM((3, 2, G, 4 * N), jnp.float32)] * 2
+    scratch += [pltpu.VMEM((3, 200, 4 * N), jnp.float32)]
+    scratch += [pltpu.VMEM(lines_table.shape, lines_table.dtype), pltpu.SemaphoreType.DMA((4,))]
     lined = call(
         line_kernel,
-        [VMEM, VMEM, HBM],
+        [VMEM, HBM, HBM],
         [chunk],
         (exchange(spread), hat, lines_table),
         scratch,
-        limit=51_000_000,
+        limit=53_300_000,
     )
     back = exchange(lined)
     kept, sent = call(

time: 85.7 us -> 83 us (0.968); the launches traced: 85.3 us -> 84.4 us
  matrix products: 0 us -> 4.78 us
  waiting for transfers between devices: 31.4 us -> 28.5 us
  local copies, waits for them, and re-layouts: 4.38 us -> 2.4 us
  Pallas kernels: 15.4 us -> 14.4 us
    dot_general x0 -> x1, matrix products: none -> 4.78 us  [local(): jnp.einsum('rx,qnx->qrn', jnp.asarray(fold_table()), kernel_hat.reshape(3...]
    all_to_all x1, waiting for transfers between devices: 12.2 us -> 9.35 us  [exchange(): lax.all_to_all(chunks, 'slab', split_axis=0, concat_axis=0, tiled=True)]
    reshape x2 -> x1, local copies, waits for them, and re-layouts: 4.36 us -> 2.38 us  [local(): kernel_hat.reshape(3, 4 * N, N)]
    pallas_call x5, Pallas kernels: 15.4 us -> 14.4 us  [call(): pl.pallas_call(kernel, out_shape=shapes if many else shapes[0], in_specs=...]
  transfers between devices with their start and end apart: 3 -> 3, of which waited for: 3 -> 3; matrix products, arithmetic and copies ran while one was open for 5% -> 8% of each run, Pallas kernels for 1% -> 1%
where the time goes in v1:
time: 83 us; the launch traced here: 84.4 us
  waiting for transfers between devices  28.5 us (34%)
  blocking collectives  18.9 us (23%)
  starting transfers between devices  14.4 us (17%)
  Pallas kernels  14.4 us (17%)
  matrix products  4.78 us (6%)
  local copies, waits for them, and re-layouts  2.4 us (3%)
  between operations  0.89 us (1%)
    ppermute x2, waiting for transfers between devices, by_mask(): return lambda given: then(lax.ppermute(given[0], 'grp', pairs), *given[1:])  19.2 us
    all_to_all x1, blocking collectives, exchange(): lax.all_to_all(chunks, 'slab', split_axis=0, concat_axis=0, tiled=True)  18.9 us
    pallas_call x5, Pallas kernels, call(): pl.pallas_call(kernel, out_shape=shapes if many else shapes[0], in_specs=...  14.4 us
    all_to_all x1, waiting for transfers between devices, exchange(): lax.all_to_all(chunks, 'slab', split_axis=0, concat_axis=0, tiled=True)  9.35 us
    ppermute x2, starting transfers between devices, by_mask(): return lambda given: then(lax.ppermute(given[0], 'grp', pairs), *given[1:])  7.39 us
    all_to_all x1, starting transfers between devices, exchange(): lax.all_to_all(chunks, 'slab', split_axis=0, concat_axis=0, tiled=True)  7.05 us
    dot_general x1, matrix products, local(): jnp.einsum('rx,qnx->qrn', jnp.asarray(fold_table()), kernel_hat.reshape(3...  4.78 us
    reshape x1, local copies, waits for them, and re-layouts, local(): kernel_hat.reshape(3, 4 * N, N)  2.38 us
  transfers between devices with their start and end apart: 3, of which 3 were waited for; matrix products, arithmetic and copies ran while one was open for 8% of the time, Pallas kernels for 1%

profile of v1, /device:TPU:0, one launch (start us, length us, event | category | flops | bytes accessed | tf_op | source)
XLA Modules:
  0.0 84.4 jit_solution(5250292326153500571)
XLA Ops:
  0.7 16.9 %conditional.2 = ((f32[864,128]{1,0:T(8,128)}, f32[1792,128]{1,0:T(8,128)})) conditional(s32[]{:T(128)} %clamp.4, (f32[864,128]{1,0:T(8,128)}, bf16[2,384,256]{2,1,0:T(8,128)(2,1)}, s32[1]{0:T(128)}) %tuple.69, (f32[864,128]{1,0:T(8,128)}, bf16[2,384,256]{2,1,0:T(8,128)(2,1)}, s32[1]{0:T(128)}) %tuple.70, ...), branch_computations={%region_0.0_spmd, %region_1.0_spmd, %region_2.0_spmd, %region_3.0_... | conditional | bytes 1769520 | solution.py:322
  0.7 4.1 %collective-permute-start.3 = (f32[864,128]{1,0:T(8,128)}, f32[864,128]{1,0:T(8,128)S(1)}, u32[]{:S(2)}, u32[]{:S(2)}) collective-permute-start(f32[864,128]{1,0:T(8,128)} %get-tuple-element.78.own_hbm), channel_id=1, source_target_pairs={{0,64},{16,80},{32,96},{48,112},{64,0},{80,16},{96,32},{112,48},{1... | collective-permute-start | bytes 1327112 | tf_op jit(solution)/shard_map/cond/branch_3_fun/ppermute | solution.py:319
  4.8 1.1 %branch_3_fun.2 = (f32[864,128]{1,0:T(8,128)S(1)}, bf16[2,384,256]{2,1,0:T(8,128)(2,1)S(1)}) custom-call(f32[864,128]{1,0:T(8,128)} %get-tuple-element.78.own_hbm, bf16[2,384,256]{2,1,0:T(8,128)(2,1)} %get-tuple-element.79.tz_hbm), custom_call_target="tpu_custom_call" | custom-call | tf_op jit(solution)/shard_map/cond/branch_3_fun/pallas_call | solution.py:304
  5.9 9.2 %collective-permute-done.3.their_ref = f32[864,128]{1,0:T(8,128)S(1)} collective-permute-done((f32[864,128]{1,0:T(8,128)}, f32[864,128]{1,0:T(8,128)S(1)}, u32[]{:S(2)}, u32[]{:S(2)}) %collective-permute-start.3) | collective-permute-done | bytes 442400 | tf_op jit(solution)/shard_map/cond/branch_3_fun/ppermute | solution.py:319
  15.1 2.4 %branch_3_fun.3 = (f32[864,128]{1,0:T(8,128)}, f32[1792,128]{1,0:T(8,128)}) custom-call(s32[1]{0:T(128)} %get-tuple-element.77.upper_ref, f32[864,128]{1,0:T(8,128)S(1)} %get-tuple-element.80.own_ref, f32[864,128]{1,0:T(8,128)S(1)} %collective-permute-done.3.their_ref, bf16[2,384,256]{2,1,0:T(8,128)(2,1)S(1)} %get-tuple-element.81.tz_ref), custom_call_target="tpu_custom_call" | custom-call | tf_op jit(solution)/shard_map/cond/branch_3_fun/pallas_call | solution.py:304
  17.5 7.0 %all-to-all-start = ((f32[16,112,128]{2,1,0:T(8,128)}), f32[16,112,128]{2,1,0:T(8,128)S(1)}, u32[]{:S(2)}, u32[]{:S(2)}) async-start(f32[16,112,128]{2,1,0:T(8,128)} %bitcast.5), calls=%async_computation | async-start | bytes 1835008 | tf_op jit(solution)/shard_map/all_to_all | solution.py:335
  24.6 0.0 copy-start.4
  24.6 2.4 %reshape.38 = f32[3,768,192]{2,1,0:T(8,128)S(1)} reshape(f32[12,36864]{1,0:T(8,128)} %param.24) | data formatting | bytes 3538944 | tf_op jit(solution)/shard_map/reshape | solution.py:370
  27.0 0.0 copy-done.4
  27.0 4.8 %convolution_bitcast_fusion.hat_hbm = f32[3,200,768]{2,1,0:T(8,128)} fusion(f32[200,192,1]{0,1,2:T(8,128)S(1)} %copy-done.4, f32[3,768,192]{2,1,0:T(8,128)S(1)} %reshape.38), kind=kOutput, calls=%fused_computation | convolution fusion | flops 1061683200 | bytes 3766272 | tf_op jit(solution)/shard_map/rx,qnx->qrn/dot_general | solution.py:367
  31.8 9.3 %all-to-all-done = f32[16,112,128]{2,1,0:T(8,128)S(1)} async-done(((f32[16,112,128]{2,1,0:T(8,128)}), f32[16,112,128]{2,1,0:T(8,128)S(1)}, u32[]{:S(2)}, u32[]{:S(2)}) %all-to-all-start) | async-done | bytes 917536 | tf_op jit(solution)/shard_map/all_to_all | solution.py:335
  41.1 0.0 copy-start
  41.1 0.0 copy-start.1
  41.1 0.0 copy-start.2
  41.1 0.0 copy-start.3
  41.1 6.7 %shard_map.82 = f32[1792,128]{1,0:T(8,128)S(1)} custom-call(f32[1792,128]{1,0:T(8,128)S(1)} %bitcast.24, f32[3,200,768]{2,1,0:T(8,128)} %convolution_bitcast_fusion.hat_hbm, bf16[2,1664,256]{2,1,0:T(8,128)(2,1)} %constant.22.clone.table_hbm), custom_call_target="tpu_custom_call" | custom-call | tf_op jit(solution)/shard_map/pallas_call | solution.py:304
  47.9 18.9 %all_to_all.10 = f32[16,112,128]{2,1,0:T(8,128)S(1)} all-to-all(f32[16,112,128]{2,1,0:T(8,128)S(1)} %bitcast.25), channel_id=1, replica_groups=mesh['grp'=8,'slab'=16] {'slab'}, dimensions={0} | all-to-all | bytes 1835008 | tf_op jit(solution)/shard_map/all_to_all | solution.py:335
  66.8 0.0 copy-done
  66.8 0.0 copy-done.1
  66.8 0.0 copy-done.2
  66.8 0.0 copy-done.3
  66.8 2.4 %shard_map.83 = (f32[864,128]{1,0:T(8,128)S(1)}, f32[872,128]{1,0:T(8,128)S(1)}) custom-call(s32[1]{0:T(128)} %bitcast.1.upper_ref, s32[2]{0:T(128)S(1)} %copy-done.1, f32[1792,128]{1,0:T(8,128)S(1)} %bitcast.23, f32[864,128]{1,0:T(8,128)S(1)} %bitcast.33, f32[864,128]{1,0:T(8,128)S(1)} %copy-done.3, bf16[2,256,384]{2,1,0:T(8,128)(2,1)S(1)} %copy-done), custom_call_target="tpu_custom_call" | custom-call | tf_op jit(solution)/shard_map/pallas_call | solution.py:304
  69.2 13.3 %conditional.3 = (f32[872,128]{1,0:T(8,128)}) conditional(s32[]{:T(128)} %clamp.4, f32[872,128]{1,0:T(8,128)S(1)} %get-tuple-element.104, f32[872,128]{1,0:T(8,128)S(1)} %get-tuple-element.104, f32[872,128]{1,0:T(8,128)S(1)} %get-tuple-element.104, f32[872,128]{1,0:T(8,128)S(1)} %get-tuple-element.104, ...), branch_computations={%region_7.0_spmd, %region_8.0_spmd, %region_9.0_spmd, %region_10.0... | conditional | bytes 1785904 | solution.py:322
  69.2 3.3 %collective-permute-start.10 = (f32[872,128]{1,0:T(8,128)S(1)}, f32[872,128]{1,0:T(8,128)}, u32[]{:S(2)}, u32[]{:S(2)}) collective-permute-start(f32[872,128]{1,0:T(8,128)S(1)} %param.10), channel_id=1, source_target_pairs={{0,64},{16,80},{32,96},{48,112},{64,0},{80,16},{96,32},{112,48},{1... | collective-permute-start | bytes 1339400 | tf_op jit(solution)/shard_map/cond/branch_3_fun/ppermute | solution.py:319
  72.5 10.0 %collective-permute-done.10 = f32[872,128]{1,0:T(8,128)} collective-permute-done((f32[872,128]{1,0:T(8,128)S(1)}, f32[872,128]{1,0:T(8,128)}, u32[]{:S(2)}, u32[]{:S(2)}) %collective-permute-start.10) | collective-permute-done | bytes 446496 | tf_op jit(solution)/shard_map/cond/branch_3_fun/ppermute | solution.py:319
  82.5 1.8 %shard_map.84 = f32[864,128]{1,0:T(8,128)} custom-call(s32[1]{0:T(128)} %bitcast.1.upper_ref, f32[864,128]{1,0:T(8,128)S(1)} %get-tuple-element.103.kept_ref, f32[872,128]{1,0:T(8,128)} %get-tuple-element.120.come_hbm), custom_call_target="tpu_custom_call" | custom-call | tf_op jit(solution)/shard_map/pallas_call | solution.py:304
Async XLA Ops:
  0.7 14.4 %collective-permute-start.3 = (f32[864,128]{1,0:T(8,128)}, f32[864,128]{1,0:T(8,128)S(1)}, u32[]{:S(2)}, u32[]{:S(2)}) collective-permute-start(f32[864,128]{1,0:T(8,128)} %get-tuple-element.78.own_hbm), channel_id=1, source_target_pairs={{0,64},{16,80},{32,96},{48,112},{64,0},{80,16},{96,32},{112,48},{1... | collective-permute-start | bytes 1327112 | tf_op jit(solution)/shard_map/cond/branch_3_fun/ppermute | solution.py:319
  17.5 23.6 %all-to-all-start = ((f32[16,112,128]{2,1,0:T(8,128)}), f32[16,112,128]{2,1,0:T(8,128)S(1)}, u32[]{:S(2)}, u32[]{:S(2)}) async-start(f32[16,112,128]{2,1,0:T(8,128)} %bitcast.5), calls=%async_computation | async-start | bytes 1835008 | tf_op jit(solution)/shard_map/all_to_all | solution.py:335
  24.6 2.4 %copy-start.4 = (f32[200,192,1]{0,1,2:T(8,128)S(1)}, f32[200,192,1]{0,1,2:T(8,128)}, u32[]{:S(2)}) copy-start(f32[200,192,1]{0,1,2:T(8,128)} %constant.28) | copy-start | bytes 460804
  41.1 25.7 %copy-start = (bf16[2,256,384]{2,1,0:T(8,128)(2,1)S(1)}, bf16[2,256,384]{2,1,0:T(8,128)(2,1)}, u32[]{:S(2)}) copy-start(bf16[2,256,384]{2,1,0:T(8,128)(2,1)} %constant.23.clone.tv_ref) | copy-start | bytes 1179652
  41.1 25.7 %copy-start.1 = (s32[2]{0:T(128)S(1)}, s32[2]{0:T(128)}, u32[]{:S(2)}) copy-start(s32[2]{0:T(128)} %occupation_ref.1) | copy-start | bytes 28
  41.1 25.7 %copy-start.2 = (f32[2,6,9216]{2,0,1:T(2,128)S(1)}, f32[2,6,9216]{2,0,1:T(2,128)}, u32[]{:S(2)}) copy-start(f32[2,6,9216]{2,0,1:T(2,128)} %param.22) | copy-start | bytes 1327108
  41.1 25.7 %copy-start.3 = (f32[864,128]{1,0:T(8,128)S(1)}, f32[864,128]{1,0:T(8,128)}, u32[]{:S(2)}) copy-start(f32[864,128]{1,0:T(8,128)} %get-tuple-element.102.their_hbm) | copy-start | bytes 1327108
  69.2 13.3 %collective-permute-start.10 = (f32[872,128]{1,0:T(8,128)S(1)}, f32[872,128]{1,0:T(8,128)}, u32[]{:S(2)}, u32[]{:S(2)}) collective-permute-start(f32[872,128]{1,0:T(8,128)S(1)} %param.10), channel_id=1, source_target_pairs={{0,64},{16,80},{32,96},{48,112},{64,0},{80,16},{96,32},{112,48},{1... | collective-permute-start | bytes 1339400 | tf_op jit(solution)/shard_map/cond/branch_3_fun/ppermute | solution.py:319

commit v2 on v1

--- a/solution.py
+++ b/solution.py
@@ -96,7 +96,15 @@
     return jnp.concatenate([rows[24 * q : 24 * q + 24] for q in range(4)], axis=1)
 
 
-def near_kernel(own_hbm, tz_hbm, own_ref, tz_ref, sems):
+def is_upper(mask):
+    return jnp.bitwise_and(lax.axis_index("grp"), 1 << (mask.bit_length() - 1)) != 0
+
+
+def near_kernel(occupation_ref, own_hbm, tz_hbm, own_ref, tz_ref, facts_ref, sems, *, mask):
+    row = lax.broadcasted_iota(jnp.int32, (8, 128), 0)
+    weight = [0.25 * occupation_ref[o].astype(jnp.float32) for o in range(2)]
+    upper = jnp.where(is_upper(mask), 1.0, 0.0)
+    facts_ref[...] = jnp.where(row == 0, weight[0], jnp.where(row == 1, weight[1], upper))
     copies = [
         pltpu.make_async_copy(own_hbm, own_ref, sems.at[0]),
         pltpu.make_async_copy(tz_hbm, tz_ref, sems.at[1]),
@@ -108,11 +116,11 @@
 
 
 def spread_kernel(
-    upper_ref, own_ref, their_ref, tz_ref, their_hbm, out_hbm, out_ref, sems, their_sem
+    own_ref, their_ref, tz_ref, their_hbm, out_hbm, out_ref, sems, their_sem, *, mask
 ):
     kept = pltpu.make_async_copy(their_ref, their_hbm, their_sem)
     kept.start()
-    upper = upper_ref[0] == 1
+    upper = is_upper(mask)
     pad = jnp.zeros((G, 32), jnp.float32)
     outs = []
     for x in range(XS):
@@ -225,14 +233,14 @@
 
 
 def term_kernel(
-    upper_ref, occupation_ref, in_ref, own_ref, their_hbm, tv_ref, kept_ref, sent_ref, their_ref,
+    in_ref, own_ref, their_hbm, facts_ref, tv_ref, kept_ref, sent_ref, their_ref,
     field_ref, sem
 ):
     fetch = pltpu.make_async_copy(their_hbm, their_ref, sem)
     fetch.start()
-    upper = upper_ref[0] == 1
+    upper = facts_ref[2:3, :1] > 0.5
     table = (tv_ref[0], tv_ref[1])
-    weight = [0.25 * occupation_ref[o].astype(jnp.float32) for o in range(2)]
+    weight = [facts_ref[o : o + 1, :1] for o in range(2)]
     for x in range(XS):
         pieces = [
             jnp.concatenate(
@@ -264,41 +272,35 @@
                 place = pl.ds(144 * x + o + 2 * tile, 24, stride=6)
                 kept_ref[place, :] = kept[o][:, 128 * tile : 128 * tile + 128]
                 sent_ref[place, :] = sent[o][:, 128 * tile : 128 * tile + 128]
-    row = lax.broadcasted_iota(jnp.int32, (8, 128), 0)
-    sent_ref[864:872, :] = jnp.where(row % 2 == 1, weight[1], weight[0])
-
-
-PARTS = ((864, 8), (0, 216), (216, 216), (432, 216), (648, 216))
-
-
-def sum_kernel(upper_ref, kept_ref, come_hbm, out_hbm, come_ref, out_ref, sems):
-    fetches, outs = [], []
-    for k, (row, count) in enumerate(PARTS):
-        place = pl.ds(row, count)
-        fetches.append(pltpu.make_async_copy(come_hbm.at[place], come_ref.at[place], sems.at[k]))
-        fetches[-1].start()
-    upper = upper_ref[0] == 1
+    sent_ref[864:872, :] = facts_ref[...]
+
+
+def sum_kernel(kept_ref, come_ref, out_hbm, out_ref, sems, *, mask):
+    upper = is_upper(mask)
     odd_row = lax.broadcasted_iota(jnp.int32, (216, 128), 0) % 2 == 1
-    fetches[0].wait()
     even = jnp.where(upper, come_ref[865:866, :], come_ref[864:865, :])
     odd = jnp.where(upper, come_ref[864:865, :], come_ref[865:866, :])
     weight = jnp.where(odd_row, odd, even)
-    for k, (row, count) in enumerate(PARTS[1:], 1):
-        place = pl.ds(row, count)
-        fetches[k].wait()
+    outs = []
+    for k in range(4):
+        place = pl.ds(216 * k, 216)
         out_ref[place, :] = -(kept_ref[place, :] * weight + come_ref[place, :])
-        outs.append(pltpu.make_async_copy(out_ref.at[place], out_hbm.at[place], sems.at[4 + k]))
+        outs.append(pltpu.make_async_copy(out_ref.at[place], out_hbm.at[place], sems.at[k]))
         outs[-1].start()
     for copy in outs:
         copy.wait()
 
 
+def same_kernel(in_hbm, out_hbm):
+    pass
+
+
 SMEM = pl.BlockSpec(memory_space=pltpu.SMEM)
 VMEM = pl.BlockSpec(memory_space=pltpu.VMEM)
 HBM = pl.BlockSpec(memory_space=pltpu.HBM)
 
 
-def call(kernel, ins, outs, args, scratch=(), out_spec=VMEM, limit=28_000_000):
+def call(kernel, ins, outs, args, scratch=(), out_spec=VMEM, limit=28_000_000, alias=None):
     shapes = [o if isinstance(o, jax.ShapeDtypeStruct) else jax.ShapeDtypeStruct(o, jnp.float32) for o in outs]
     many = len(shapes) > 1
     return pl.pallas_call(
@@ -307,16 +309,17 @@
         in_specs=ins,
         out_specs=[out_spec] * len(outs) if many else out_spec,
         scratch_shapes=scratch,
+        input_output_aliases=alias or {},
         compiler_params=pltpu.CompilerParams(vmem_limit_bytes=limit),
     )(*args)
 
 
-def to_partner(value, pair_bits, then=lambda come: come, *others):
+def to_partner(value, pair_bits, then, *others):
     group_count = lax.axis_size("grp")
 
     def by_mask(mask):
         pairs = [(source, source ^ mask) for source in range(group_count)]
-        return lambda given: then(lax.ppermute(given[0], "grp", pairs), *given[1:])
+        return lambda given: then(mask, lax.ppermute(given[0], "grp", pairs), *given[1:])
 
     branches = [by_mask(mask) for mask in range(1, group_count)]
     return lax.switch(pair_bits - 1, branches, (value, *others))
@@ -348,22 +351,26 @@
 def local(orbitals, occupation, kernel_hat, pair_mask):
     tz, lines_table, tv = [jnp.asarray(t) for t in tables()]
     pair_bits = pair_mask[0]
-    own_group = lax.axis_index("grp")
-    upper = (own_group > jnp.bitwise_xor(own_group, pair_bits)).astype(jnp.int32).reshape(1)
     own = to_rows(orbitals)
     chunk = (SLABS * ROWS, 128)
     rows = pltpu.VMEM((864, 128), jnp.float32)
 
-    def spread_out(theirs, own, upper, tz):
+    def spread_out(mask, theirs, own, occupation, tz):
         near = [jax.ShapeDtypeStruct(a.shape, a.dtype) for a in (own, tz)]
-        own, tz = call(near_kernel, [HBM] * 2, near, (own, tz), [pltpu.SemaphoreType.DMA((2,))])
+        own, tz, facts = call(
+            functools.partial(near_kernel, mask=mask),
+            [SMEM, HBM, HBM],
+            near + [(8, 128)],
+            (occupation, own, tz),
+            [pltpu.SemaphoreType.DMA((2,))],
+        )
         scratch = [pltpu.VMEM(chunk, jnp.float32), pltpu.SemaphoreType.DMA((2 * SLABS,))]
         scratch.append(pltpu.SemaphoreType.DMA)
-        operands = (upper, own, theirs, tz)
+        kernel = functools.partial(spread_kernel, mask=mask)
         outs = [(864, 128), chunk]
-        return call(spread_kernel, [SMEM] + [VMEM] * 3, outs, operands, scratch, HBM)
-
-    theirs, spread = to_partner(own, pair_bits, spread_out, own, upper, tz)
+        return *call(kernel, [VMEM] * 3, outs, (own, theirs, tz), scratch, HBM), facts
+
+    theirs, spread, facts = to_partner(own, pair_bits, spread_out, own, occupation, tz)
     hat = jnp.einsum(
         "rx,qnx->qrn",
         jnp.asarray(fold_table()),
@@ -384,16 +391,21 @@
     back = exchange(lined)
     kept, sent = call(
         term_kernel,
-        [SMEM, SMEM, VMEM, VMEM, HBM, VMEM],
+        [VMEM, VMEM, HBM, VMEM, VMEM],
         [(864, 128), (872, 128)],
-        (upper, occupation, back, own, theirs, tv),
+        (back, own, theirs, facts, tv),
         [rows, pltpu.VMEM((2, XS, 24, 384), jnp.float32), pltpu.SemaphoreType.DMA],
     )
 
-    come = to_partner(sent, pair_bits)
-    scratch = [pltpu.VMEM((872, 128), jnp.float32), rows, pltpu.SemaphoreType.DMA((9,))]
-    total = call(sum_kernel, [SMEM, VMEM, HBM], [(864, 128)], (upper, kept, come), scratch, HBM)
-    return from_rows(total)
+    def total(mask, come, kept):
+        kernel = functools.partial(sum_kernel, mask=mask)
+        scratch = [rows, pltpu.SemaphoreType.DMA((4,))]
+        return call(kernel, [VMEM] * 2, [(864, 128)], (kept, come), scratch, HBM)
+
+    out = to_partner(sent, pair_bits, total, kept)
+    return from_rows(
+        call(same_kernel, [HBM], [(864, 128)], (out,), (), HBM, limit=66_800_000, alias={0: 0})
+    )
 
 
 def solution(mesh):

time: 83 us -> 83.5 us (level); the launches traced: 84.4 us -> 83.2 us
    pallas_call x5 -> x6, Pallas kernels: 14.4 us -> 14 us  [call(): pl.pallas_call(kernel, out_shape=shapes if many else shapes[0], in_specs=...]
  transfers between devices with their start and end apart: 3 -> 3, of which waited for: 3 -> 3; matrix products, arithmetic and copies ran while one was open for 8% -> 9% of each run, Pallas kernels for 1% -> 2%
where the time goes in v2:
time: 83.5 us; the launch traced here: 83.2 us
  waiting for transfers between devices  27.8 us (33%)
  blocking collectives  18.9 us (23%)
  starting transfers between devices  14.4 us (17%)
  Pallas kernels  14 us (17%)
  matrix products  4.79 us (6%)
  local copies, waits for them, and re-layouts  2.39 us (3%)
  between operations  0.88 us (1%)
    all_to_all x1, blocking collectives, exchange(): lax.all_to_all(chunks, 'slab', split_axis=0, concat_axis=0, tiled=True)  18.9 us
    ppermute x2, waiting for transfers between devices, by_mask(): lax.ppermute(given[0], 'grp', pairs)  18.4 us
    pallas_call x6, Pallas kernels, call(): pl.pallas_call(kernel, out_shape=shapes if many else shapes[0], in_specs=...  14 us
    all_to_all x1, waiting for transfers between devices, exchange(): lax.all_to_all(chunks, 'slab', split_axis=0, concat_axis=0, tiled=True)  9.34 us
    ppermute x2, starting transfers between devices, by_mask(): lax.ppermute(given[0], 'grp', pairs)  7.39 us
    all_to_all x1, starting transfers between devices, exchange(): lax.all_to_all(chunks, 'slab', split_axis=0, concat_axis=0, tiled=True)  7.05 us
    dot_general x1, matrix products, local(): jnp.einsum('rx,qnx->qrn', jnp.asarray(fold_table()), kernel_hat.reshape(3...  4.79 us
    reshape x1, local copies, waits for them, and re-layouts, local(): kernel_hat.reshape(3, 4 * N, N)  2.38 us
  transfers between devices with their start and end apart: 3, of which 3 were waited for; matrix products, arithmetic and copies ran while one was open for 9% of the time, Pallas kernels for 2%

profile of v2, /device:TPU:0, one launch (start us, length us, event | category | flops | bytes accessed | tf_op | source)
XLA Modules:
  0.0 83.2 jit_solution(7328983287378053847)
XLA Ops:
  0.7 16.9 %conditional.2 = (f32[864,128]{1,0:T(8,128)}, f32[1792,128]{1,0:T(8,128)}, f32[8,128]{1,0:T(8,128)S(1)}) conditional(s32[]{:T(128)} %bitcast, (s32[2]{0:T(128)}, f32[864,128]{1,0:T(8,128)}, bf16[2,384,256]{2,1,0:T(8,128)(2,1)}) %tuple.70, (s32[2]{0:T(128)}, f32[864,128]{1,0:T(8,128)}, ...), branch_computations={%region_0.0_spmd, %region_1.0_spmd, %region_2.0_spmd, %region_3.0_... | conditional | bytes 1769536 | solution.py:325
  0.7 4.1 %collective-permute-start.3 = (f32[864,128]{1,0:T(8,128)}, f32[864,128]{1,0:T(8,128)S(1)}, u32[]{:S(2)}, u32[]{:S(2)}) collective-permute-start(f32[864,128]{1,0:T(8,128)} %get-tuple-element.108.own_hbm), channel_id=1, source_target_pairs={{0,64},{16,80},{32,96},{48,112},{64,0},{80,16},{96,32},{112,48},{1... | collective-permute-start | bytes 1327112 | tf_op jit(solution)/shard_map/cond/branch_3_fun/ppermute | solution.py:322
  4.8 1.8 %branch_3_fun.3 = (f32[864,128]{1,0:T(8,128)S(1)}, bf16[2,384,256]{2,1,0:T(8,128)(2,1)S(1)}, f32[8,128]{1,0:T(8,128)S(1)}) custom-call(s32[2]{0:T(128)} %get-tuple-element.107.occupation_ref, f32[864,128]{1,0:T(8,128)} %get-tuple-element.108.own_hbm, bf16[2,384,256]{2,1,0:T(8,128)(2,1)} %get-tuple-element.109.tz_hbm), custom_call_target="tpu_custom_call" | custom-call | tf_op jit(solution)/shard_map/cond/branch_3_fun/pallas_call | solution.py:306
  6.6 8.6 %collective-permute-done.3.their_ref = f32[864,128]{1,0:T(8,128)S(1)} collective-permute-done((f32[864,128]{1,0:T(8,128)}, f32[864,128]{1,0:T(8,128)S(1)}, u32[]{:S(2)}, u32[]{:S(2)}) %collective-permute-start.3) | collective-permute-done | bytes 442400 | tf_op jit(solution)/shard_map/cond/branch_3_fun/ppermute | solution.py:322
  15.1 2.4 %branch_3_fun.4 = (f32[864,128]{1,0:T(8,128)}, f32[1792,128]{1,0:T(8,128)}) custom-call(f32[864,128]{1,0:T(8,128)S(1)} %get-tuple-element.110.own_ref, f32[864,128]{1,0:T(8,128)S(1)} %collective-permute-done.3.their_ref, bf16[2,384,256]{2,1,0:T(8,128)(2,1)S(1)} %get-tuple-element.111.tz_ref), custom_call_target="tpu_custom_call" | custom-call | tf_op jit(solution)/shard_map/cond/branch_3_fun/pallas_call | solution.py:306
  17.5 7.1 %all-to-all-start = ((f32[16,112,128]{2,1,0:T(8,128)}), f32[16,112,128]{2,1,0:T(8,128)S(1)}, u32[]{:S(2)}, u32[]{:S(2)}) async-start(f32[16,112,128]{2,1,0:T(8,128)} %bitcast.4), calls=%async_computation | async-start | bytes 1835008 | tf_op jit(solution)/shard_map/all_to_all | solution.py:338
  24.6 0.0 copy-start.2
  24.6 2.4 %reshape.36 = f32[3,768,192]{2,1,0:T(8,128)S(1)} reshape(f32[12,36864]{1,0:T(8,128)} %param.24) | data formatting | bytes 3538944 | tf_op jit(solution)/shard_map/reshape | solution.py:377
  27.0 0.0 copy-done.2
  27.0 4.8 %convolution_bitcast_fusion.hat_hbm = f32[3,200,768]{2,1,0:T(8,128)} fusion(f32[200,192,1]{0,1,2:T(8,128)S(1)} %copy-done.2, f32[3,768,192]{2,1,0:T(8,128)S(1)} %reshape.36), kind=kOutput, calls=%fused_computation | convolution fusion | flops 1061683200 | bytes 3766272 | tf_op jit(solution)/shard_map/rx,qnx->qrn/dot_general | solution.py:374
  31.8 9.3 %all-to-all-done = f32[16,112,128]{2,1,0:T(8,128)S(1)} async-done(((f32[16,112,128]{2,1,0:T(8,128)}), f32[16,112,128]{2,1,0:T(8,128)S(1)}, u32[]{:S(2)}, u32[]{:S(2)}) %all-to-all-start) | async-done | bytes 917536 | tf_op jit(solution)/shard_map/all_to_all | solution.py:338
  41.1 0.0 copy-start
  41.1 0.0 copy-start.1
  41.1 6.7 %shard_map.82 = f32[1792,128]{1,0:T(8,128)S(1)} custom-call(f32[1792,128]{1,0:T(8,128)S(1)} %bitcast.21, f32[3,200,768]{2,1,0:T(8,128)} %convolution_bitcast_fusion.hat_hbm, bf16[2,1664,256]{2,1,0:T(8,128)(2,1)} %constant.19.clone.table_hbm), custom_call_target="tpu_custom_call" | custom-call | tf_op jit(solution)/shard_map/pallas_call | solution.py:306
  47.8 18.9 %all_to_all.10 = f32[16,112,128]{2,1,0:T(8,128)S(1)} all-to-all(f32[16,112,128]{2,1,0:T(8,128)S(1)} %bitcast.22), channel_id=1, replica_groups=mesh['grp'=8,'slab'=16] {'slab'}, dimensions={0} | all-to-all | bytes 1835008 | tf_op jit(solution)/shard_map/all_to_all | solution.py:338
  66.7 0.0 copy-done
  66.7 0.0 copy-done.1
  66.7 2.3 %shard_map.83 = (f32[864,128]{1,0:T(8,128)S(1)}, f32[872,128]{1,0:T(8,128)S(1)}) custom-call(f32[1792,128]{1,0:T(8,128)S(1)} %bitcast.20, f32[864,128]{1,0:T(8,128)S(1)} %bitcast.30, f32[864,128]{1,0:T(8,128)} %get-tuple-element.159.their_hbm, f32[8,128]{1,0:T(8,128)S(1)} %get-tuple-element.160.facts_ref, bf16[2,256,384]{2,1,0:T(8,128)(2,1)S(1)} %copy-done), custom_call_target="tpu_custom_call" | custom-call | tf_op jit(solution)/shard_map/pallas_call | solution.py:306
  69.0 14.1 %conditional.3 = (f32[864,128]{1,0:T(8,128)}) conditional(s32[]{:T(128)} %bitcast, (f32[872,128]{1,0:T(8,128)S(1)}, f32[864,128]{1,0:T(8,128)S(1)}) %tuple.55, (f32[872,128]{1,0:T(8,128)S(1)}, f32[864,128]{1,0:T(8,128)S(1)}) %tuple.55, (f32[872,128]{1,0:T(8,128)S(1)}, f32[864,128]{1,0:T(8,128)S(1)}) %tuple.55, ...), branch_computations={%region_7.0_spmd, %region_8.0_spmd, %region_9.0_spmd, %region_10.0... | conditional | bytes 1785904 | solution.py:325
  69.0 3.3 %collective-permute-start.10 = (f32[872,128]{1,0:T(8,128)S(1)}, f32[872,128]{1,0:T(8,128)S(1)}, u32[]{:S(2)}, u32[]{:S(2)}) collective-permute-start(f32[872,128]{1,0:T(8,128)S(1)} %get-tuple-element.146), channel_id=1, source_target_pairs={{0,64},{16,80},{32,96},{48,112},{64,0},{80,16},{96,32},{112,48},{1... | collective-permute-start | bytes 1339400 | tf_op jit(solution)/shard_map/cond/branch_3_fun/ppermute | solution.py:322
  72.4 9.9 %collective-permute-done.10.come_ref = f32[872,128]{1,0:T(8,128)S(1)} collective-permute-done((f32[872,128]{1,0:T(8,128)S(1)}, f32[872,128]{1,0:T(8,128)S(1)}, u32[]{:S(2)}, u32[]{:S(2)}) %collective-permute-start.10) | collective-permute-done | bytes 446496 | tf_op jit(solution)/shard_map/cond/branch_3_fun/ppermute | solution.py:322
  82.2 0.8 branch_3_fun.5
  (1 shorter events, 0.0 us)
Async XLA Ops:
  0.7 14.4 %collective-permute-start.3 = (f32[864,128]{1,0:T(8,128)}, f32[864,128]{1,0:T(8,128)S(1)}, u32[]{:S(2)}, u32[]{:S(2)}) collective-permute-start(f32[864,128]{1,0:T(8,128)} %get-tuple-element.108.own_hbm), channel_id=1, source_target_pairs={{0,64},{16,80},{32,96},{48,112},{64,0},{80,16},{96,32},{112,48},{1... | collective-permute-start | bytes 1327112 | tf_op jit(solution)/shard_map/cond/branch_3_fun/ppermute | solution.py:322
  17.5 23.6 %all-to-all-start = ((f32[16,112,128]{2,1,0:T(8,128)}), f32[16,112,128]{2,1,0:T(8,128)S(1)}, u32[]{:S(2)}, u32[]{:S(2)}) async-start(f32[16,112,128]{2,1,0:T(8,128)} %bitcast.4), calls=%async_computation | async-start | bytes 1835008 | tf_op jit(solution)/shard_map/all_to_all | solution.py:338
  24.6 2.4 %copy-start.2 = (f32[200,192,1]{0,1,2:T(8,128)S(1)}, f32[200,192,1]{0,1,2:T(8,128)}, u32[]{:S(2)}) copy-start(f32[200,192,1]{0,1,2:T(8,128)} %constant.25) | copy-start | bytes 460804
  41.1 25.6 %copy-start = (bf16[2,256,384]{2,1,0:T(8,128)(2,1)S(1)}, bf16[2,256,384]{2,1,0:T(8,128)(2,1)}, u32[]{:S(2)}) copy-start(bf16[2,256,384]{2,1,0:T(8,128)(2,1)} %constant.20.clone.tv_ref) | copy-start | bytes 1179652
  41.1 25.6 %copy-start.1 = (f32[2,6,9216]{2,0,1:T(2,128)S(1)}, f32[2,6,9216]{2,0,1:T(2,128)}, u32[]{:S(2)}) copy-start(f32[2,6,9216]{2,0,1:T(2,128)} %param.22) | copy-start | bytes 1327108
  69.0 13.2 %collective-permute-start.10 = (f32[872,128]{1,0:T(8,128)S(1)}, f32[872,128]{1,0:T(8,128)S(1)}, u32[]{:S(2)}, u32[]{:S(2)}) collective-permute-start(f32[872,128]{1,0:T(8,128)S(1)} %get-tuple-element.146), channel_id=1, source_target_pairs={{0,64},{16,80},{32,96},{48,112},{64,0},{80,16},{96,32},{112,48},{1... | collective-permute-start | bytes 1339400 | tf_op jit(solution)/shard_map/cond/branch_3_fun/ppermute | solution.py:322

commit v3 on v2

--- a/solution.py
+++ b/solution.py
@@ -172,64 +172,83 @@
     def table(row, count, columns=256):
         return [table_ref[part, row : row + count, :columns] for part in range(2)]
 
-    pieces = []
-    for kp in range(KP):
-        for x in range(XS):
-            pieces.append(
-                jnp.concatenate(
-                    [
-                        in_ref[pl.ds(18 * x + 6 * tile + kp, SLABS, stride=ROWS), :]
-                        for tile in range(3)
-                    ],
-                    axis=1,
-                )
-            )
-    data = split(jnp.concatenate(pieces, axis=0))
+    def gathered(kps):
+        pieces = []
+        for kp in kps:
+            for x in range(XS):
+                place = [pl.ds(18 * x + 6 * tile + kp, SLABS, stride=ROWS) for tile in range(3)]
+                pieces.append(jnp.concatenate([in_ref[p, :] for p in place], axis=1))
+        return split(jnp.concatenate(pieces, axis=0))
+
+    def y_forward(q, data):
+        for c in range(2):
+            result = []
+            for kz2 in range(2):
+                window = [part[:, 128 * kz2 : 128 * kz2 + 256] for part in data]
+                result.append(mm(window, table(WY + 320 * c + 64 * (1 - kz2), 256)))
+            paired = side_by_side(*result)
+            for half in range(2):
+                y_ref[q, c, :, 384 * half : 384 * half + 384] = paired[96 * half : 96 * half + 96]
+
+    data = gathered((0, 1))
     fetches[0].wait()
-    for c in range(2):
-        result = []
-        for kz2 in range(2):
-            window = [part[:, 128 * kz2 : 128 * kz2 + 256] for part in data]
-            result.append(mm(window, table(WY + 320 * c + 64 * (1 - kz2), 256)))
-        paired = side_by_side(*result)
-        for kp in range(KP):
-            lanes = slice(384 * (kp % 2), 384 * (kp % 2) + 384)
-            y_ref[kp // 2, c, :, lanes] = paired[96 * kp : 96 * kp + 96]
-    fetches[1].wait()
-    fetches[2].wait()
-    first_row = lax.broadcasted_iota(jnp.int32, (G, 768), 0) == 0
     for q in range(3):
-        forward = table(TX, N, G)
-        re = mm(forward, split(y_ref[q, 0]))
-        im = mm(forward, split(y_ref[q, 1]))
-        even, odd = hat_ref[q, :G], hat_ref[q, G:N]
-        even_sin = jnp.where(first_row, hat_ref[q, N : N + 1], even)
+        coming = gathered((2 * q + 2, 2 * q + 3)) if q < 2 else None
+        y_forward(q, data)
+        data = coming
+    for copy in fetches[1:]:
+        copy.wait()
+    first_row = lax.broadcasted_iota(jnp.int32, (G, 256), 0) == 0
+    forward = table(TX, N, G)
+
+    def spectra(i):
+        q, hl = places[i]
+        return [mm(forward, split(y_ref[q, c, :, hl])) for c in range(2)]
+
+    def multiplied(i, re, im):
+        q, hl = places[i]
+        even, odd = hat_ref[q, :G, hl], hat_ref[q, G:N, hl]
+        even_sin = jnp.where(first_row, hat_ref[q, N : N + 1, hl], even)
         cos_re = even * re[:G] + odd * im[G:]
         sin_im = odd * im[:G] - even_sin * re[G:]
         cos_im = even * im[:G] - odd * re[G:]
         sin_re = odd * re[:G] + even_sin * im[G:]
-        u_ref[q, 0] = mm(table(TI, G, N), split(jnp.concatenate([cos_re, sin_im], axis=0)))
-        u_ref[q, 1] = mm(table(TI + G, G, N), split(jnp.concatenate([cos_im, sin_re], axis=0)))
-    fetches[3].wait()
-    sides = []
-    for kz2 in range(2):
-        parts = []
-        for c in range(2):
-            rows = []
-            for kp in range(KP):
-                lane = 384 * (kp % 2) + 128 * kz2
-                rows.append(u_ref[kp // 2, c, :, lane : lane + 256])
-            back = split(jnp.concatenate(rows, axis=0))
-            parts.append(mm(back, table(WI + 320 * c + 64 * (1 - kz2), 256)))
-        sides.append(parts[0] + parts[1])
-    wide = side_by_side(*sides)
-    for kp in range(KP):
-        for x in range(XS):
-            for tile in range(3):
-                row = 96 * kp + 16 * x
-                out_ref[pl.ds(18 * x + 6 * tile + kp, SLABS, stride=ROWS), :] = wide[
-                    row : row + 16, 128 * tile : 128 * tile + 128
-                ]
+        return (
+            split(jnp.concatenate([cos_re, sin_im], axis=0)),
+            split(jnp.concatenate([cos_im, sin_re], axis=0)),
+        )
+
+    def back(i, first, second):
+        q, hl = places[i]
+        u_ref[q, 0, :, hl] = mm(table(TI, G, N), first)
+        u_ref[q, 1, :, hl] = mm(table(TI + G, G, N), second)
+    def y_back(q):
+        sides = []
+        for kz2 in range(2):
+            parts = []
+            for c in range(2):
+                lane = [384 * half + 128 * kz2 for half in range(2)]
+                rows = [u_ref[q, c, :, first : first + 256] for first in lane]
+                window = split(jnp.concatenate(rows, axis=0))
+                parts.append(mm(window, table(WI + 320 * c + 64 * (1 - kz2), 256)))
+            sides.append(parts[0] + parts[1])
+        wide = side_by_side(*sides)
+        for half in range(2):
+            for x in range(XS):
+                row = 96 * half + 16 * x
+                for tile in range(3):
+                    place = pl.ds(18 * x + 6 * tile + 2 * q + half, SLABS, stride=ROWS)
+                    out_ref[place, :] = wide[row : row + 16, 128 * tile : 128 * tile + 128]
+
+    places = [(q, slice(w, w + 256)) for q in range(3) for w in range(0, 768, 256)]
+    ahead = [spectra(i) for i in range(2)]
+    for i in range(len(places)):
+        product = multiplied(i, *ahead.pop(0))
+        if i + 2 < len(places):
+            ahead.append(spectra(i + 2))
+        back(i, *product)
+    for q in range(3):
+        y_back(q)
 
 
 def term_kernel(

time: 83.5 us -> 82.6 us (0.989)
  no operation moved by 1% of the time
where the time goes in v3:
time: 82.6 us; the launch traced here: 82.3 us
  waiting for transfers between devices  27.8 us (34%)
  blocking collectives  18.9 us (23%)
  starting transfers between devices  14.3 us (17%)
  Pallas kernels  13.2 us (16%)
  matrix products  4.79 us (6%)
  local copies, waits for them, and re-layouts  2.39 us (3%)
  between operations  0.88 us (1%)
    all_to_all x1, blocking collectives, exchange(): lax.all_to_all(chunks, 'slab', split_axis=0, concat_axis=0, tiled=True)  18.9 us
    ppermute x2, waiting for transfers between devices, by_mask(): lax.ppermute(given[0], 'grp', pairs)  18.4 us
    pallas_call x6, Pallas kernels, call(): pl.pallas_call(kernel, out_shape=shapes if many else shapes[0], in_specs=...  13.2 us
    all_to_all x1, waiting for transfers between devices, exchange(): lax.all_to_all(chunks, 'slab', split_axis=0, concat_axis=0, tiled=True)  9.34 us
    ppermute x2, starting transfers between devices, by_mask(): lax.ppermute(given[0], 'grp', pairs)  7.25 us
    all_to_all x1, starting transfers between devices, exchange(): lax.all_to_all(chunks, 'slab', split_axis=0, concat_axis=0, tiled=True)  7.05 us
    dot_general x1, matrix products, local(): jnp.einsum('rx,qnx->qrn', jnp.asarray(fold_table()), kernel_hat.reshape(3...  4.79 us
    reshape x1, local copies, waits for them, and re-layouts, local(): kernel_hat.reshape(3, 4 * N, N)  2.38 us
  transfers between devices with their start and end apart: 3, of which 3 were waited for; matrix products, arithmetic and copies ran while one was open for 9% of the time, Pallas kernels for 2%

profile of v3, /device:TPU:0, one launch (start us, length us, event | category | flops | bytes accessed | tf_op | source)
XLA Modules:
  0.0 82.3 jit_solution(8066326153015349400)
XLA Ops:
  0.7 17.0 %conditional.2 = (f32[864,128]{1,0:T(8,128)}, f32[1792,128]{1,0:T(8,128)}, f32[8,128]{1,0:T(8,128)S(1)}) conditional(s32[]{:T(128)} %bitcast, (s32[2]{0:T(128)}, f32[864,128]{1,0:T(8,128)}, bf16[2,384,256]{2,1,0:T(8,128)(2,1)}) %tuple.70, (s32[2]{0:T(128)}, f32[864,128]{1,0:T(8,128)}, ...), branch_computations={%region_0.0_spmd, %region_1.0_spmd, %region_2.0_spmd, %region_3.0_... | conditional | bytes 1769536 | solution.py:344
  0.7 4.2 %collective-permute-start.5 = (f32[864,128]{1,0:T(8,128)}, f32[864,128]{1,0:T(8,128)S(1)}, u32[]{:S(2)}, u32[]{:S(2)}) collective-permute-start(f32[864,128]{1,0:T(8,128)} %get-tuple-element.124.own_hbm), channel_id=1, source_target_pairs={{0,96},{16,112},{32,64},{48,80},{64,32},{80,48},{96,0},{112,16},{1... | collective-permute-start | bytes 1327112 | tf_op jit(solution)/shard_map/cond/branch_5_fun/ppermute | solution.py:341
  4.9 1.8 %branch_5_fun.3 = (f32[864,128]{1,0:T(8,128)S(1)}, bf16[2,384,256]{2,1,0:T(8,128)(2,1)S(1)}, f32[8,128]{1,0:T(8,128)S(1)}) custom-call(s32[2]{0:T(128)} %get-tuple-element.123.occupation_ref, f32[864,128]{1,0:T(8,128)} %get-tuple-element.124.own_hbm, bf16[2,384,256]{2,1,0:T(8,128)(2,1)} %get-tuple-element.125.tz_hbm), custom_call_target="tpu_custom_call" | custom-call | tf_op jit(solution)/shard_map/cond/branch_5_fun/pallas_call | solution.py:325
  6.7 8.6 %collective-permute-done.5.their_ref = f32[864,128]{1,0:T(8,128)S(1)} collective-permute-done((f32[864,128]{1,0:T(8,128)}, f32[864,128]{1,0:T(8,128)S(1)}, u32[]{:S(2)}, u32[]{:S(2)}) %collective-permute-start.5) | collective-permute-done | bytes 442400 | tf_op jit(solution)/shard_map/cond/branch_5_fun/ppermute | solution.py:341
  15.3 2.4 %branch_5_fun.4 = (f32[864,128]{1,0:T(8,128)}, f32[1792,128]{1,0:T(8,128)}) custom-call(f32[864,128]{1,0:T(8,128)S(1)} %get-tuple-element.126.own_ref, f32[864,128]{1,0:T(8,128)S(1)} %collective-permute-done.5.their_ref, bf16[2,384,256]{2,1,0:T(8,128)(2,1)S(1)} %get-tuple-element.127.tz_ref), custom_call_target="tpu_custom_call" | custom-call | tf_op jit(solution)/shard_map/cond/branch_5_fun/pallas_call | solution.py:325
  17.7 7.1 %all-to-all-start = ((f32[16,112,128]{2,1,0:T(8,128)}), f32[16,112,128]{2,1,0:T(8,128)S(1)}, u32[]{:S(2)}, u32[]{:S(2)}) async-start(f32[16,112,128]{2,1,0:T(8,128)} %bitcast.4), calls=%async_computation | async-start | bytes 1835008 | tf_op jit(solution)/shard_map/all_to_all | solution.py:357
  24.7 0.0 copy-start.2
  24.8 2.4 %reshape.36 = f32[3,768,192]{2,1,0:T(8,128)S(1)} reshape(f32[12,36864]{1,0:T(8,128)} %param.24) | data formatting | bytes 3538944 | tf_op jit(solution)/shard_map/reshape | solution.py:396
  27.1 0.0 copy-done.2
  27.2 4.8 %convolution_bitcast_fusion.hat_hbm = f32[3,200,768]{2,1,0:T(8,128)} fusion(f32[200,192,1]{0,1,2:T(8,128)S(1)} %copy-done.2, f32[3,768,192]{2,1,0:T(8,128)S(1)} %reshape.36), kind=kOutput, calls=%fused_computation | convolution fusion | flops 1061683200 | bytes 3766272 | tf_op jit(solution)/shard_map/rx,qnx->qrn/dot_general | solution.py:393
  31.9 9.3 %all-to-all-done = f32[16,112,128]{2,1,0:T(8,128)S(1)} async-done(((f32[16,112,128]{2,1,0:T(8,128)}), f32[16,112,128]{2,1,0:T(8,128)S(1)}, u32[]{:S(2)}, u32[]{:S(2)}) %all-to-all-start) | async-done | bytes 917536 | tf_op jit(solution)/shard_map/all_to_all | solution.py:357
  41.3 0.0 copy-start
  41.3 0.0 copy-start.1
  41.3 5.9 %shard_map.82 = f32[1792,128]{1,0:T(8,128)S(1)} custom-call(f32[1792,128]{1,0:T(8,128)S(1)} %bitcast.21, f32[3,200,768]{2,1,0:T(8,128)} %convolution_bitcast_fusion.hat_hbm, bf16[2,1664,256]{2,1,0:T(8,128)(2,1)} %constant.19.clone.table_hbm), custom_call_target="tpu_custom_call" | custom-call | tf_op jit(solution)/shard_map/pallas_call | solution.py:325
  47.2 18.9 %all_to_all.10 = f32[16,112,128]{2,1,0:T(8,128)S(1)} all-to-all(f32[16,112,128]{2,1,0:T(8,128)S(1)} %bitcast.22), channel_id=1, replica_groups=mesh['grp'=8,'slab'=16] {'slab'}, dimensions={0} | all-to-all | bytes 1835008 | tf_op jit(solution)/shard_map/all_to_all | solution.py:357
  66.1 0.0 copy-done
  66.1 0.0 copy-done.1
  66.1 2.3 %shard_map.83 = (f32[864,128]{1,0:T(8,128)S(1)}, f32[872,128]{1,0:T(8,128)S(1)}) custom-call(f32[1792,128]{1,0:T(8,128)S(1)} %bitcast.20, f32[864,128]{1,0:T(8,128)S(1)} %bitcast.30, f32[864,128]{1,0:T(8,128)} %get-tuple-element.159.their_hbm, f32[8,128]{1,0:T(8,128)S(1)} %get-tuple-element.160.facts_ref, bf16[2,256,384]{2,1,0:T(8,128)(2,1)S(1)} %copy-done), custom_call_target="tpu_custom_call" | custom-call | tf_op jit(solution)/shard_map/pallas_call | solution.py:325
  68.4 13.8 %conditional.3 = (f32[864,128]{1,0:T(8,128)}) conditional(s32[]{:T(128)} %bitcast, (f32[872,128]{1,0:T(8,128)S(1)}, f32[864,128]{1,0:T(8,128)S(1)}) %tuple.55, (f32[872,128]{1,0:T(8,128)S(1)}, f32[864,128]{1,0:T(8,128)S(1)}) %tuple.55, (f32[872,128]{1,0:T(8,128)S(1)}, f32[864,128]{1,0:T(8,128)S(1)}) %tuple.55, ...), branch_computations={%region_7.0_spmd, %region_8.0_spmd, %region_9.0_spmd, %region_10.0... | conditional | bytes 1785904 | solution.py:344
  68.4 3.0 %collective-permute-start.12 = (f32[872,128]{1,0:T(8,128)S(1)}, f32[872,128]{1,0:T(8,128)S(1)}, u32[]{:S(2)}, u32[]{:S(2)}) collective-permute-start(f32[872,128]{1,0:T(8,128)S(1)} %get-tuple-element.150), channel_id=1, source_target_pairs={{0,96},{16,112},{32,64},{48,80},{64,32},{80,48},{96,0},{112,16},{1... | collective-permute-start | bytes 1339400 | tf_op jit(solution)/shard_map/cond/branch_5_fun/ppermute | solution.py:341
  71.4 9.9 %collective-permute-done.12.come_ref = f32[872,128]{1,0:T(8,128)S(1)} collective-permute-done((f32[872,128]{1,0:T(8,128)S(1)}, f32[872,128]{1,0:T(8,128)S(1)}, u32[]{:S(2)}, u32[]{:S(2)}) %collective-permute-start.12) | collective-permute-done | bytes 446496 | tf_op jit(solution)/shard_map/cond/branch_5_fun/ppermute | solution.py:341
  81.3 0.8 branch_5_fun.5
  (1 shorter events, 0.0 us)
Async XLA Ops:
  0.7 14.6 %collective-permute-start.5 = (f32[864,128]{1,0:T(8,128)}, f32[864,128]{1,0:T(8,128)S(1)}, u32[]{:S(2)}, u32[]{:S(2)}) collective-permute-start(f32[864,128]{1,0:T(8,128)} %get-tuple-element.124.own_hbm), channel_id=1, source_target_pairs={{0,96},{16,112},{32,64},{48,80},{64,32},{80,48},{96,0},{112,16},{1... | collective-permute-start | bytes 1327112 | tf_op jit(solution)/shard_map/cond/branch_5_fun/ppermute | solution.py:341
  17.7 23.6 %all-to-all-start = ((f32[16,112,128]{2,1,0:T(8,128)}), f32[16,112,128]{2,1,0:T(8,128)S(1)}, u32[]{:S(2)}, u32[]{:S(2)}) async-start(f32[16,112,128]{2,1,0:T(8,128)} %bitcast.4), calls=%async_computation | async-start | bytes 1835008 | tf_op jit(solution)/shard_map/all_to_all | solution.py:357
  24.7 2.4 %copy-start.2 = (f32[200,192,1]{0,1,2:T(8,128)S(1)}, f32[200,192,1]{0,1,2:T(8,128)}, u32[]{:S(2)}) copy-start(f32[200,192,1]{0,1,2:T(8,128)} %constant.25) | copy-start | bytes 460804
  41.3 24.8 %copy-start = (bf16[2,256,384]{2,1,0:T(8,128)(2,1)S(1)}, bf16[2,256,384]{2,1,0:T(8,128)(2,1)}, u32[]{:S(2)}) copy-start(bf16[2,256,384]{2,1,0:T(8,128)(2,1)} %constant.20.clone.tv_ref) | copy-start | bytes 1179652
  41.3 24.8 %copy-start.1 = (f32[2,6,9216]{2,0,1:T(2,128)S(1)}, f32[2,6,9216]{2,0,1:T(2,128)}, u32[]{:S(2)}) copy-start(f32[2,6,9216]{2,0,1:T(2,128)} %param.22) | copy-start | bytes 1327108
  68.4 12.9 %collective-permute-start.12 = (f32[872,128]{1,0:T(8,128)S(1)}, f32[872,128]{1,0:T(8,128)S(1)}, u32[]{:S(2)}, u32[]{:S(2)}) collective-permute-start(f32[872,128]{1,0:T(8,128)S(1)} %get-tuple-element.150), channel_id=1, source_target_pairs={{0,96},{16,112},{32,64},{48,80},{64,32},{80,48},{96,0},{112,16},{1... | collective-permute-start | bytes 1339400 | tf_op jit(solution)/shard_map/cond/branch_5_fun/ppermute | solution.py:341

commit v4 on v3

--- a/solution.py
+++ b/solution.py
@@ -123,25 +123,36 @@
     upper = is_upper(mask)
     pad = jnp.zeros((G, 32), jnp.float32)
     outs = []
-    for x in range(XS):
+
+    def density(x):
         theirs = [plane(their_ref, x, o) for o in range(2)]
         first = jnp.where(upper, theirs[1], theirs[0])
         second = jnp.where(upper, theirs[0], theirs[1])
         one = lines(plane(own_ref, x, 0) * first)
         two = lines(plane(own_ref, x, 1) * second)
-        density = jnp.concatenate([one, pad, two, pad], axis=1)
-        lined = mm((tz_ref[0], tz_ref[1]), split(density), (1, 1))
+        return split(jnp.concatenate([one, pad, two, pad], axis=1))
+
+    def spectra(x):
+        parts = [density(x), density(x + 1)]
+        both = [jnp.concatenate([part[k] for part in parts], axis=0) for k in range(2)]
+        return mm((tz_ref[0], tz_ref[1]), both, (1, 1))
+
+    def stored(x, lined):
         wide = jnp.concatenate([lined[96 * j : 96 * j + 96] for j in range(4)], axis=1)
         for kp in range(KP):
             for tile in range(3):
                 out_ref[pl.ds(18 * x + 6 * tile + kp, SLABS, stride=ROWS), :] = wide[
                     16 * kp : 16 * kp + 16, 128 * tile : 128 * tile + 128
                 ]
-        if x in (3, 5):
-            first_row, count = (0, 72) if x == 3 else (72, 40)
-            if x == 5:
-                for slab in range(SLABS):
-                    out_ref[ROWS * slab + 108 : ROWS * slab + 112, :] = jnp.zeros((4, 128), jnp.float32)
+
+    for slab in range(SLABS):
+        out_ref[ROWS * slab + 108 : ROWS * slab + 112, :] = jnp.zeros((4, 128), jnp.float32)
+    for x in range(0, XS, 2):
+        lined = spectra(x)
+        stored(x, lined[:, :96])
+        stored(x + 1, lined[:, 96:192])
+        if x in (2, 4):
+            first_row, count = (0, 72) if x == 2 else (72, 40)
             for slab in range(SLABS):
                 place = pl.ds(ROWS * slab + first_row, count)
                 outs.append(
@@ -169,6 +180,7 @@
     fetches.insert(2, pltpu.make_async_copy(hat_hbm, hat_ref, sems.at[3]))
     for copy in fetches:
         copy.start()
+
     def table(row, count, columns=256):
         return [table_ref[part, row : row + count, :columns] for part in range(2)]
 
@@ -222,6 +234,7 @@
         q, hl = places[i]
         u_ref[q, 0, :, hl] = mm(table(TI, G, N), first)
         u_ref[q, 1, :, hl] = mm(table(TI + G, G, N), second)
+
     def y_back(q):
         sides = []
         for kz2 in range(2):
@@ -260,7 +273,8 @@
     upper = facts_ref[2:3, :1] > 0.5
     table = (tv_ref[0], tv_ref[1])
     weight = [facts_ref[o : o + 1, :1] for o in range(2)]
-    for x in range(XS):
+
+    def gathered(x):
         pieces = [
             jnp.concatenate(
                 [
@@ -271,11 +285,20 @@
             )
             for kp in range(KP)
         ]
-        wide = jnp.concatenate(pieces, axis=0)
-        stacked = jnp.concatenate([wide[:, 96 * j : 96 * j + 96] for j in range(4)], axis=0)
-        fields = mm(table, split(stacked)).T
-        field_ref[0, x] = dense_of(fields[:, :96])
-        field_ref[1, x] = dense_of(fields[:, 128:224])
+        return jnp.concatenate(pieces, axis=0)
+
+    def spectrum(x):
+        pair = (gathered(x), gathered(x + 1))
+        lanes = [slice(96 * j, 96 * j + 96) for j in range(4)]
+        both = [jnp.concatenate([wide[:, part] for wide in pair], axis=1) for part in lanes]
+        return split(jnp.concatenate(both, axis=0))
+
+    for x in range(0, XS, 2):
+        fields = mm(table, spectrum(x)).T
+        for k in range(2):
+            rows = fields[96 * k : 96 * k + 96]
+            field_ref[0, x + k] = dense_of(rows[:, :96])
+            field_ref[1, x + k] = dense_of(rows[:, 128:224])
     fetch.wait()
     for x in range(XS):
         one, two = field_ref[0, x], field_ref[1, x]

time: 82.6 us -> 80.5 us (0.975); the launches traced: 82.3 us -> 82 us
  no operation moved by 1% of the time
where the time goes in v4:
time: 80.5 us; the launch traced here: 82 us
  waiting for transfers between devices  27.8 us (35%)
  blocking collectives  18.9 us (23%)
  starting transfers between devices  14.4 us (18%)
  Pallas kernels  12.7 us (16%)
  matrix products  4.79 us (6%)
  local copies, waits for them, and re-layouts  2.39 us (3%)
  between operations  0.88 us (1%)
    all_to_all x1, blocking collectives, exchange(): lax.all_to_all(chunks, 'slab', split_axis=0, concat_axis=0, tiled=True)  18.9 us
    ppermute x2, waiting for transfers between devices, by_mask(): lax.ppermute(given[0], 'grp', pairs)  18.4 us
    pallas_call x6, Pallas kernels, call(): pl.pallas_call(kernel, out_shape=shapes if many else shapes[0], in_specs=...  12.7 us
    all_to_all x1, waiting for transfers between devices, exchange(): lax.all_to_all(chunks, 'slab', split_axis=0, concat_axis=0, tiled=True)  9.34 us
    ppermute x2, starting transfers between devices, by_mask(): lax.ppermute(given[0], 'grp', pairs)  7.39 us
    all_to_all x1, starting transfers between devices, exchange(): lax.all_to_all(chunks, 'slab', split_axis=0, concat_axis=0, tiled=True)  7.06 us
    dot_general x1, matrix products, local(): jnp.einsum('rx,qnx->qrn', jnp.asarray(fold_table()), kernel_hat.reshape(3...  4.79 us
    reshape x1, local copies, waits for them, and re-layouts, local(): kernel_hat.reshape(3, 4 * N, N)  2.38 us
  transfers between devices with their start and end apart: 3, of which 3 were waited for; matrix products, arithmetic and copies ran while one was open for 9% of the time, Pallas kernels for 2%

profile of v4, /device:TPU:0, one launch (start us, length us, event | category | flops | bytes accessed | tf_op | source)
XLA Modules:
  0.0 82.0 jit_solution(5935043155436616878)
XLA Ops:
  0.7 16.7 %conditional.2 = (f32[864,128]{1,0:T(8,128)}, f32[1792,128]{1,0:T(8,128)}, f32[8,128]{1,0:T(8,128)S(1)}) conditional(s32[]{:T(128)} %bitcast, (s32[2]{0:T(128)}, f32[864,128]{1,0:T(8,128)}, bf16[2,384,256]{2,1,0:T(8,128)(2,1)}) %tuple.70, (s32[2]{0:T(128)}, f32[864,128]{1,0:T(8,128)}, ...), branch_computations={%region_0.0_spmd, %region_1.0_spmd, %region_2.0_spmd, %region_3.0_... | conditional | bytes 1769536 | solution.py:367
  0.7 4.1 %collective-permute-start.3 = (f32[864,128]{1,0:T(8,128)}, f32[864,128]{1,0:T(8,128)S(1)}, u32[]{:S(2)}, u32[]{:S(2)}) collective-permute-start(f32[864,128]{1,0:T(8,128)} %get-tuple-element.108.own_hbm), channel_id=1, source_target_pairs={{0,64},{16,80},{32,96},{48,112},{64,0},{80,16},{96,32},{112,48},{1... | collective-permute-start | bytes 1327112 | tf_op jit(solution)/shard_map/cond/branch_3_fun/ppermute | solution.py:364
  4.8 1.8 %branch_3_fun.3 = (f32[864,128]{1,0:T(8,128)S(1)}, bf16[2,384,256]{2,1,0:T(8,128)(2,1)S(1)}, f32[8,128]{1,0:T(8,128)S(1)}) custom-call(s32[2]{0:T(128)} %get-tuple-element.107.occupation_ref, f32[864,128]{1,0:T(8,128)} %get-tuple-element.108.own_hbm, bf16[2,384,256]{2,1,0:T(8,128)(2,1)} %get-tuple-element.109.tz_hbm), custom_call_target="tpu_custom_call" | custom-call | tf_op jit(solution)/shard_map/cond/branch_3_fun/pallas_call | solution.py:348
  6.6 8.6 %collective-permute-done.3.their_ref = f32[864,128]{1,0:T(8,128)S(1)} collective-permute-done((f32[864,128]{1,0:T(8,128)}, f32[864,128]{1,0:T(8,128)S(1)}, u32[]{:S(2)}, u32[]{:S(2)}) %collective-permute-start.3) | collective-permute-done | bytes 442400 | tf_op jit(solution)/shard_map/cond/branch_3_fun/ppermute | solution.py:364
  15.1 2.2 %branch_3_fun.4 = (f32[864,128]{1,0:T(8,128)}, f32[1792,128]{1,0:T(8,128)}) custom-call(f32[864,128]{1,0:T(8,128)S(1)} %get-tuple-element.110.own_ref, f32[864,128]{1,0:T(8,128)S(1)} %collective-permute-done.3.their_ref, bf16[2,384,256]{2,1,0:T(8,128)(2,1)S(1)} %get-tuple-element.111.tz_ref), custom_call_target="tpu_custom_call" | custom-call | tf_op jit(solution)/shard_map/cond/branch_3_fun/pallas_call | solution.py:348
  17.4 7.1 %all-to-all-start = ((f32[16,112,128]{2,1,0:T(8,128)}), f32[16,112,128]{2,1,0:T(8,128)S(1)}, u32[]{:S(2)}, u32[]{:S(2)}) async-start(f32[16,112,128]{2,1,0:T(8,128)} %bitcast.4), calls=%async_computation | async-start | bytes 1835008 | tf_op jit(solution)/shard_map/all_to_all | solution.py:380
  24.4 0.0 copy-start.2
  24.4 2.4 %reshape.36 = f32[3,768,192]{2,1,0:T(8,128)S(1)} reshape(f32[12,36864]{1,0:T(8,128)} %param.24) | data formatting | bytes 3538944 | tf_op jit(solution)/shard_map/reshape | solution.py:419
  26.8 0.0 copy-done.2
  26.8 4.8 %convolution_bitcast_fusion.hat_hbm = f32[3,200,768]{2,1,0:T(8,128)} fusion(f32[200,192,1]{0,1,2:T(8,128)S(1)} %copy-done.2, f32[3,768,192]{2,1,0:T(8,128)S(1)} %reshape.36), kind=kOutput, calls=%fused_computation | convolution fusion | flops 1061683200 | bytes 3766272 | tf_op jit(solution)/shard_map/rx,qnx->qrn/dot_general | solution.py:416
  31.6 9.3 %all-to-all-done = f32[16,112,128]{2,1,0:T(8,128)S(1)} async-done(((f32[16,112,128]{2,1,0:T(8,128)}), f32[16,112,128]{2,1,0:T(8,128)S(1)}, u32[]{:S(2)}, u32[]{:S(2)}) %all-to-all-start) | async-done | bytes 917536 | tf_op jit(solution)/shard_map/all_to_all | solution.py:380
  41.0 0.0 copy-start
  41.0 0.0 copy-start.1
  41.0 5.9 %shard_map.82 = f32[1792,128]{1,0:T(8,128)S(1)} custom-call(f32[1792,128]{1,0:T(8,128)S(1)} %bitcast.21, f32[3,200,768]{2,1,0:T(8,128)} %convolution_bitcast_fusion.hat_hbm, bf16[2,1664,256]{2,1,0:T(8,128)(2,1)} %constant.19.clone.table_hbm), custom_call_target="tpu_custom_call" | custom-call | tf_op jit(solution)/shard_map/pallas_call | solution.py:348
  46.9 18.9 %all_to_all.10 = f32[16,112,128]{2,1,0:T(8,128)S(1)} all-to-all(f32[16,112,128]{2,1,0:T(8,128)S(1)} %bitcast.22), channel_id=1, replica_groups=mesh['grp'=8,'slab'=16] {'slab'}, dimensions={0} | all-to-all | bytes 1835008 | tf_op jit(solution)/shard_map/all_to_all | solution.py:380
  65.8 0.0 copy-done
  65.8 0.0 copy-done.1
  65.8 1.9 %shard_map.83 = (f32[864,128]{1,0:T(8,128)S(1)}, f32[872,128]{1,0:T(8,128)S(1)}) custom-call(f32[1792,128]{1,0:T(8,128)S(1)} %bitcast.20, f32[864,128]{1,0:T(8,128)S(1)} %bitcast.30, f32[864,128]{1,0:T(8,128)} %get-tuple-element.159.their_hbm, f32[8,128]{1,0:T(8,128)S(1)} %get-tuple-element.160.facts_ref, bf16[2,256,384]{2,1,0:T(8,128)(2,1)S(1)} %copy-done), custom_call_target="tpu_custom_call" | custom-call | tf_op jit(solution)/shard_map/pallas_call | solution.py:348
  67.7 14.1 %conditional.3 = (f32[864,128]{1,0:T(8,128)}) conditional(s32[]{:T(128)} %bitcast, (f32[872,128]{1,0:T(8,128)S(1)}, f32[864,128]{1,0:T(8,128)S(1)}) %tuple.55, (f32[872,128]{1,0:T(8,128)S(1)}, f32[864,128]{1,0:T(8,128)S(1)}) %tuple.55, (f32[872,128]{1,0:T(8,128)S(1)}, f32[864,128]{1,0:T(8,128)S(1)}) %tuple.55, ...), branch_computations={%region_7.0_spmd, %region_8.0_spmd, %region_9.0_spmd, %region_10.0... | conditional | bytes 1785904 | solution.py:367
  67.8 3.3 %collective-permute-start.10 = (f32[872,128]{1,0:T(8,128)S(1)}, f32[872,128]{1,0:T(8,128)S(1)}, u32[]{:S(2)}, u32[]{:S(2)}) collective-permute-start(f32[872,128]{1,0:T(8,128)S(1)} %get-tuple-element.146), channel_id=1, source_target_pairs={{0,64},{16,80},{32,96},{48,112},{64,0},{80,16},{96,32},{112,48},{1... | collective-permute-start | bytes 1339400 | tf_op jit(solution)/shard_map/cond/branch_3_fun/ppermute | solution.py:364
  71.1 9.9 %collective-permute-done.10.come_ref = f32[872,128]{1,0:T(8,128)S(1)} collective-permute-done((f32[872,128]{1,0:T(8,128)S(1)}, f32[872,128]{1,0:T(8,128)S(1)}, u32[]{:S(2)}, u32[]{:S(2)}) %collective-permute-start.10) | collective-permute-done | bytes 446496 | tf_op jit(solution)/shard_map/cond/branch_3_fun/ppermute | solution.py:364
  80.9 0.8 %branch_3_fun.5 = f32[864,128]{1,0:T(8,128)} custom-call(f32[864,128]{1,0:T(8,128)S(1)} %get-tuple-element.145.kept_ref, f32[872,128]{1,0:T(8,128)S(1)} %collective-permute-done.10.come_ref), custom_call_target="tpu_custom_call" | custom-call | tf_op jit(solution)/shard_map/cond/branch_3_fun/pallas_call | solution.py:348
  (1 shorter events, 0.0 us)
Async XLA Ops:
  0.7 14.4 %collective-permute-start.3 = (f32[864,128]{1,0:T(8,128)}, f32[864,128]{1,0:T(8,128)S(1)}, u32[]{:S(2)}, u32[]{:S(2)}) collective-permute-start(f32[864,128]{1,0:T(8,128)} %get-tuple-element.108.own_hbm), channel_id=1, source_target_pairs={{0,64},{16,80},{32,96},{48,112},{64,0},{80,16},{96,32},{112,48},{1... | collective-permute-start | bytes 1327112 | tf_op jit(solution)/shard_map/cond/branch_3_fun/ppermute | solution.py:364
  17.4 23.6 %all-to-all-start = ((f32[16,112,128]{2,1,0:T(8,128)}), f32[16,112,128]{2,1,0:T(8,128)S(1)}, u32[]{:S(2)}, u32[]{:S(2)}) async-start(f32[16,112,128]{2,1,0:T(8,128)} %bitcast.4), calls=%async_computation | async-start | bytes 1835008 | tf_op jit(solution)/shard_map/all_to_all | solution.py:380
  24.4 2.4 %copy-start.2 = (f32[200,192,1]{0,1,2:T(8,128)S(1)}, f32[200,192,1]{0,1,2:T(8,128)}, u32[]{:S(2)}) copy-start(f32[200,192,1]{0,1,2:T(8,128)} %constant.25) | copy-start | bytes 460804
  41.0 24.8 %copy-start = (bf16[2,256,384]{2,1,0:T(8,128)(2,1)S(1)}, bf16[2,256,384]{2,1,0:T(8,128)(2,1)}, u32[]{:S(2)}) copy-start(bf16[2,256,384]{2,1,0:T(8,128)(2,1)} %constant.20.clone.tv_ref) | copy-start | bytes 1179652
  41.0 24.8 %copy-start.1 = (f32[2,6,9216]{2,0,1:T(2,128)S(1)}, f32[2,6,9216]{2,0,1:T(2,128)}, u32[]{:S(2)}) copy-start(f32[2,6,9216]{2,0,1:T(2,128)} %param.22) | copy-start | bytes 1327108
  67.8 13.2 %collective-permute-start.10 = (f32[872,128]{1,0:T(8,128)S(1)}, f32[872,128]{1,0:T(8,128)S(1)}, u32[]{:S(2)}, u32[]{:S(2)}) collective-permute-start(f32[872,128]{1,0:T(8,128)S(1)} %get-tuple-element.146), channel_id=1, source_target_pairs={{0,64},{16,80},{32,96},{48,112},{64,0},{80,16},{96,32},{112,48},{1... | collective-permute-start | bytes 1339400 | tf_op jit(solution)/shard_map/cond/branch_3_fun/ppermute | solution.py:364

commit v5 on v4

--- a/solution.py
+++ b/solution.py
@@ -116,13 +116,12 @@
 
 
 def spread_kernel(
-    own_ref, their_ref, tz_ref, their_hbm, out_hbm, out_ref, sems, their_sem, *, mask
+    own_ref, their_ref, tz_ref, their_hbm, out_ref, their_sem, *, mask
 ):
     kept = pltpu.make_async_copy(their_ref, their_hbm, their_sem)
     kept.start()
     upper = is_upper(mask)
     pad = jnp.zeros((G, 32), jnp.float32)
-    outs = []
 
     def density(x):
         theirs = [plane(their_ref, x, o) for o in range(2)]
@@ -151,16 +150,6 @@
         lined = spectra(x)
         stored(x, lined[:, :96])
         stored(x + 1, lined[:, 96:192])
-        if x in (2, 4):
-            first_row, count = (0, 72) if x == 2 else (72, 40)
-            for slab in range(SLABS):
-                place = pl.ds(ROWS * slab + first_row, count)
-                outs.append(
-                    pltpu.make_async_copy(out_ref.at[place], out_hbm.at[place], sems.at[len(outs)])
-                )
-                outs[-1].start()
-    for copy in outs:
-        copy.wait()
     kept.wait()
 
 
@@ -349,7 +338,7 @@
         kernel,
         out_shape=shapes if many else shapes[0],
         in_specs=ins,
-        out_specs=[out_spec] * len(outs) if many else out_spec,
+        out_specs=(out_spec if isinstance(out_spec, list) else [out_spec] * len(outs)) if many else out_spec,
         scratch_shapes=scratch,
         input_output_aliases=alias or {},
         compiler_params=pltpu.CompilerParams(vmem_limit_bytes=limit),
@@ -379,6 +368,22 @@
     chunks = chunks.reshape(SLABS, ROWS, 128)
     moved = lax.all_to_all(chunks, "slab", split_axis=0, concat_axis=0, tiled=True)
     return moved.reshape(SLABS * ROWS, 128)
+
+
+def fold_kernel(fold_ref, hat_ref, out_ref):
+    def one_group(q, carry):
+        rest = hat_ref[q]
+        total = jnp.zeros((200, 4 * N), jnp.float32)
+        for _ in range(3):
+            part = rest.astype(jnp.bfloat16)
+            rest = rest - part.astype(jnp.float32)
+            total = total + lax.dot_general(
+                fold_ref[...], part, (((1,), (1,)), ((), ())), preferred_element_type=jnp.float32
+            )
+        out_ref[q] = total
+        return carry
+
+    lax.fori_loop(0, 3, one_group, 0)
 
 
 def fold_table():
@@ -397,7 +402,7 @@
     chunk = (SLABS * ROWS, 128)
     rows = pltpu.VMEM((864, 128), jnp.float32)
 
-    def spread_out(mask, theirs, own, occupation, tz):
+    def spread_out(mask, theirs, own, occupation, tz, kernel_hat, fold):
         near = [jax.ShapeDtypeStruct(a.shape, a.dtype) for a in (own, tz)]
         own, tz, facts = call(
             functools.partial(near_kernel, mask=mask),
@@ -406,18 +411,17 @@
             (occupation, own, tz),
             [pltpu.SemaphoreType.DMA((2,))],
         )
-        scratch = [pltpu.VMEM(chunk, jnp.float32), pltpu.SemaphoreType.DMA((2 * SLABS,))]
-        scratch.append(pltpu.SemaphoreType.DMA)
         kernel = functools.partial(spread_kernel, mask=mask)
         outs = [(864, 128), chunk]
-        return *call(kernel, [VMEM] * 3, outs, (own, theirs, tz), scratch, HBM), facts
-
-    theirs, spread, facts = to_partner(own, pair_bits, spread_out, own, occupation, tz)
-    hat = jnp.einsum(
-        "rx,qnx->qrn",
-        jnp.asarray(fold_table()),
-        kernel_hat.reshape(3, 4 * N, N),
-        precision=lax.Precision.HIGHEST,
+        scratch = [pltpu.SemaphoreType.DMA]
+        spread = call(kernel, [VMEM] * 3, outs, (own, theirs, tz), scratch, [HBM, VMEM])
+        lines = kernel_hat.reshape(3, 4 * N, N)
+        hat = call(fold_kernel, [VMEM] * 2, [(3, 200, 4 * N)], (fold, lines))
+        return *spread, facts, hat
+
+    fold = jnp.asarray(fold_table(), jnp.bfloat16)
+    theirs, spread, facts, hat = to_partner(
+        own, pair_bits, spread_out, own, occupation, tz, kernel_hat, fold
     )
     scratch = [pltpu.VMEM((3, 2, G, 4 * N), jnp.float32)] * 2
     scratch += [pltpu.VMEM((3, 200, 4 * N), jnp.float32)]

time: 80.5 us -> 80.4 us (level)
  blocking collectives: 18.9 us -> 42.2 us
  waiting for transfers between devices: 27.8 us -> 14.3 us
  starting transfers between devices: 14.4 us -> 7.26 us
  matrix products: 4.79 us -> 0 us
    all_to_all x1 -> x2, blocking collectives: 18.9 us -> 42.2 us  [exchange(): lax.all_to_all(chunks, 'slab', split_axis=0, concat_axis=0, tiled=True)]
    all_to_all x1 -> x0, waiting for transfers between devices: 9.34 us -> none  [exchange(): lax.all_to_all(chunks, 'slab', split_axis=0, concat_axis=0, tiled=True)]
    all_to_all x1 -> x0, starting transfers between devices: 7.06 us -> none  [exchange(): lax.all_to_all(chunks, 'slab', split_axis=0, concat_axis=0, tiled=True)]
    dot_general x1 -> x0, matrix products: 4.79 us -> none  [local(): jnp.einsum('rx,qnx->qrn', jnp.asarray(fold_table()), kernel_hat.reshape(3...]
    ppermute x2, waiting for transfers between devices: 18.4 us -> 14.3 us  [by_mask(): lax.ppermute(given[0], 'grp', pairs)]
    pallas_call x6 -> x7, Pallas kernels: 12.7 us -> 13.4 us  [call(): pl.pallas_call(kernel, out_shape=shapes if many else shapes[0], in_specs=...]
  transfers between devices with their start and end apart: 3 -> 2, of which waited for: 3 -> 2; matrix products, arithmetic and copies ran while one was open for 9% -> 3% of each run, Pallas kernels for 2% -> 4%
where the time goes in v5:
time: 80.4 us; the launch traced here: 81.1 us
  blocking collectives  42.2 us (52%)
  waiting for transfers between devices  14.3 us (18%)
  Pallas kernels  13.4 us (17%)
  starting transfers between devices  7.26 us (9%)
  local copies, waits for them, and re-layouts  2.43 us (3%)
  between operations  0.92 us (1%)
    all_to_all x2, blocking collectives, exchange(): lax.all_to_all(chunks, 'slab', split_axis=0, concat_axis=0, tiled=True)  42.2 us
    ppermute x2, waiting for transfers between devices, by_mask(): lax.ppermute(given[0], 'grp', pairs)  14.3 us
    pallas_call x7, Pallas kernels, call(): pl.pallas_call(kernel, out_shape=shapes if many else shapes[0], in_specs=...  13.4 us
    ppermute x2, starting transfers between devices, by_mask(): lax.ppermute(given[0], 'grp', pairs)  7.26 us
    reshape x1, local copies, waits for them, and re-layouts, spread_out(): lines = kernel_hat.reshape(3, 4 * N, N)  2.4 us
  transfers between devices with their start and end apart: 2, of which 2 were waited for; matrix products, arithmetic and copies ran while one was open for 3% of the time, Pallas kernels for 4%

profile of v5, /device:TPU:0, one launch (start us, length us, event | category | flops | bytes accessed | tf_op | source)
XLA Modules:
  0.0 81.1 jit_solution(16631904652982874448)
XLA Ops:
  0.7 16.8 %conditional.2 = (f32[864,128]{1,0:T(8,128)}, f32[1792,128]{1,0:T(8,128)S(1)}, f32[8,128]{1,0:T(8,128)S(1)}, f32[3,200,768]{2,1,0:T(8,128)S(1)}) conditional(s32[]{:T(128)} %bitcast, (s32[2]{0:T(128)}, f32[864,128]{1,0:T(8,128)}, bf16[2,384,256]{2,1,0:T(8,128)(2,1)}, f32[12,36864]{1,0:T(8,128)}, ...), branch_computations={%region_0.0_spmd, %region_1.0_spmd, %region_2.0_spmd, %region_3.0_... | conditional | bytes 7385276 | solution.py:356
  0.9 4.2 %collective-permute-start.5 = (f32[864,128]{1,0:T(8,128)}, f32[864,128]{1,0:T(8,128)S(1)}, u32[]{:S(2)}, u32[]{:S(2)}) collective-permute-start(f32[864,128]{1,0:T(8,128)} %get-tuple-element.162.own_hbm), channel_id=1, source_target_pairs={{0,96},{16,112},{32,64},{48,80},{64,32},{80,48},{96,0},{112,16},{1... | collective-permute-start | bytes 1327112 | tf_op jit(solution)/shard_map/cond/branch_5_fun/ppermute | solution.py:353
  5.1 0.0 copy-start.7
  5.1 0.0 copy-start.23
  5.1 0.0 copy-start.15
  5.1 2.4 %reshape.40.hat_ref = f32[3,768,192]{2,1,0:T(8,128)S(1)} reshape(f32[12,36864]{1,0:T(8,128)} %get-tuple-element.170) | data formatting | bytes 3538944 | tf_op jit(solution)/shard_map/cond/branch_5_fun/reshape | solution.py:418
  7.6 0.0 copy-done.7
  7.6 0.0 copy-done.23
  7.6 1.8 %branch_5_fun.4 = (f32[864,128]{1,0:T(8,128)S(1)}, bf16[2,384,256]{2,1,0:T(8,128)(2,1)S(1)}, f32[8,128]{1,0:T(8,128)S(1)}) custom-call(s32[2]{0:T(128)S(1)} %copy-done.23, f32[864,128]{1,0:T(8,128)S(1)} %copy-done.7, bf16[2,384,256]{2,1,0:T(8,128)(2,1)} %get-tuple-element.163.tz_hbm), custom_call_target="tpu_custom_call" | custom-call | tf_op jit(solution)/shard_map/cond/branch_5_fun/pallas_call | solution.py:337
  9.4 0.0 copy-done.15
  9.4 1.7 %branch_5_fun.6 = f32[3,200,768]{2,1,0:T(8,128)S(1)} custom-call(bf16[200,192]{1,0:T(8,128)(2,1)S(1)} %copy-done.15, f32[3,768,192]{2,1,0:T(8,128)S(1)} %reshape.40.hat_ref), custom_call_target="tpu_custom_call" | custom-call | tf_op jit(solution)/shard_map/cond/branch_5_fun/pallas_call | solution.py:337
  11.1 4.4 %collective-permute-done.5.their_ref = f32[864,128]{1,0:T(8,128)S(1)} collective-permute-done((f32[864,128]{1,0:T(8,128)}, f32[864,128]{1,0:T(8,128)S(1)}, u32[]{:S(2)}, u32[]{:S(2)}) %collective-permute-start.5) | collective-permute-done | bytes 442400 | tf_op jit(solution)/shard_map/cond/branch_5_fun/ppermute | solution.py:353
  15.5 1.6 %branch_5_fun.5 = (f32[864,128]{1,0:T(8,128)}, f32[1792,128]{1,0:T(8,128)S(1)}) custom-call(f32[864,128]{1,0:T(8,128)S(1)} %get-tuple-element.164.own_ref, f32[864,128]{1,0:T(8,128)S(1)} %collective-permute-done.5.their_ref, bf16[2,384,256]{2,1,0:T(8,128)(2,1)S(1)} %get-tuple-element.165.tz_ref), custom_call_target="tpu_custom_call" | custom-call | tf_op jit(solution)/shard_map/cond/branch_5_fun/pallas_call | solution.py:337
  17.4 0.0 copy-start.9
  17.5 23.1 %all_to_all.10 = f32[16,112,128]{2,1,0:T(8,128)S(1)} all-to-all(f32[16,112,128]{2,1,0:T(8,128)S(1)} %bitcast.26), channel_id=1, replica_groups=mesh['grp'=8,'slab'=16] {'slab'}, dimensions={0} | all-to-all | bytes 1835008 | tf_op jit(solution)/shard_map/all_to_all | solution.py:369
  40.6 0.0 copy-done.9
  40.6 5.8 %shard_map.82 = f32[1792,128]{1,0:T(8,128)S(1)} custom-call(f32[1792,128]{1,0:T(8,128)S(1)} %bitcast.16, f32[3,200,768]{2,1,0:T(8,128)} %copy-done.9, bf16[2,1664,256]{2,1,0:T(8,128)(2,1)} %constant.19.clone.table_hbm), custom_call_target="tpu_custom_call" | custom-call | tf_op jit(solution)/shard_map/pallas_call | solution.py:337
  46.4 0.0 copy-start
  46.4 0.0 copy-start.1
  46.5 0.0 copy-start.17
  46.5 19.0 %all_to_all.11 = f32[16,112,128]{2,1,0:T(8,128)S(1)} all-to-all(f32[16,112,128]{2,1,0:T(8,128)S(1)} %bitcast.17), channel_id=1, replica_groups=mesh['grp'=8,'slab'=16] {'slab'}, dimensions={0} | all-to-all | bytes 1835008 | tf_op jit(solution)/shard_map/all_to_all | solution.py:369
  65.5 0.0 copy-done
  65.5 0.0 copy-done.1
  65.5 0.0 copy-done.17
  65.5 1.6 %shard_map.83 = (f32[864,128]{1,0:T(8,128)S(1)}, f32[872,128]{1,0:T(8,128)S(1)}) custom-call(f32[1792,128]{1,0:T(8,128)S(1)} %bitcast.15, f32[864,128]{1,0:T(8,128)S(1)} %bitcast.25, f32[864,128]{1,0:T(8,128)S(1)} %copy-done.17, f32[8,128]{1,0:T(8,128)S(1)} %get-tuple-element.204.facts_ref, bf16[2,256,384]{2,1,0:T(8,128)(2,1)S(1)} %copy-done), custom_call_target="tpu_custom_call" | custom-call | tf_op jit(solution)/shard_map/pallas_call | solution.py:337
  67.1 13.8 %conditional.3 = (f32[864,128]{1,0:T(8,128)}) conditional(s32[]{:T(128)} %bitcast, (f32[872,128]{1,0:T(8,128)S(1)}, f32[864,128]{1,0:T(8,128)S(1)}) %tuple.55, (f32[872,128]{1,0:T(8,128)S(1)}, f32[864,128]{1,0:T(8,128)S(1)}) %tuple.55, (f32[872,128]{1,0:T(8,128)S(1)}, f32[864,128]{1,0:T(8,128)S(1)}) %tuple.55, ...), branch_computations={%region_7.0_spmd, %region_8.0_spmd, %region_9.0_spmd, %region_10.0... | conditional | bytes 1785904 | solution.py:356
  67.1 3.0 %collective-permute-start.12 = (f32[872,128]{1,0:T(8,128)S(1)}, f32[872,128]{1,0:T(8,128)S(1)}, u32[]{:S(2)}, u32[]{:S(2)}) collective-permute-start(f32[872,128]{1,0:T(8,128)S(1)} %get-tuple-element.192), channel_id=1, source_target_pairs={{0,96},{16,112},{32,64},{48,80},{64,32},{80,48},{96,0},{112,16},{1... | collective-permute-start | bytes 1339400 | tf_op jit(solution)/shard_map/cond/branch_5_fun/ppermute | solution.py:353
  70.2 9.9 %collective-permute-done.12.come_ref = f32[872,128]{1,0:T(8,128)S(1)} collective-permute-done((f32[872,128]{1,0:T(8,128)S(1)}, f32[872,128]{1,0:T(8,128)S(1)}, u32[]{:S(2)}, u32[]{:S(2)}) %collective-permute-start.12) | collective-permute-done | bytes 446496 | tf_op jit(solution)/shard_map/cond/branch_5_fun/ppermute | solution.py:353
  80.0 0.8 %branch_5_fun.7 = f32[864,128]{1,0:T(8,128)} custom-call(f32[864,128]{1,0:T(8,128)S(1)} %get-tuple-element.191.kept_ref, f32[872,128]{1,0:T(8,128)S(1)} %collective-permute-done.12.come_ref), custom_call_target="tpu_custom_call" | custom-call | tf_op jit(solution)/shard_map/cond/branch_5_fun/pallas_call | solution.py:337
  (1 shorter events, 0.0 us)
Async XLA Ops:
  0.9 14.6 %collective-permute-start.5 = (f32[864,128]{1,0:T(8,128)}, f32[864,128]{1,0:T(8,128)S(1)}, u32[]{:S(2)}, u32[]{:S(2)}) collective-permute-start(f32[864,128]{1,0:T(8,128)} %get-tuple-element.162.own_hbm), channel_id=1, source_target_pairs={{0,96},{16,112},{32,64},{48,80},{64,32},{80,48},{96,0},{112,16},{1... | collective-permute-start | bytes 1327112 | tf_op jit(solution)/shard_map/cond/branch_5_fun/ppermute | solution.py:353
  5.1 2.4 %copy-start.7 = (f32[864,128]{1,0:T(8,128)S(1)}, f32[864,128]{1,0:T(8,128)}, u32[]{:S(2)}) copy-start(f32[864,128]{1,0:T(8,128)} %get-tuple-element.162.own_hbm) | copy-start | bytes 1327108 | tf_op jit(solution)/shard_map/cond
  5.1 2.4 %copy-start.23 = (s32[2]{0:T(128)S(1)}, s32[2]{0:T(128)}, u32[]{:S(2)}) copy-start(s32[2]{0:T(128)} %get-tuple-element.161.occupation_ref) | copy-start | bytes 28 | tf_op jit(solution)/shard_map/cond
  5.1 4.3 %copy-start.15 = (bf16[200,192]{1,0:T(8,128)(2,1)S(1)}, bf16[200,192]{1,0:T(8,128)(2,1)}, u32[]{:S(2)}) copy-start(bf16[200,192]{1,0:T(8,128)(2,1)} %get-tuple-element.169.fold_ref) | copy-start | bytes 230404 | tf_op jit(solution)/shard_map/cond
  17.4 23.1 %copy-start.9 = (f32[3,200,768]{2,1,0:T(8,128)}, f32[3,200,768]{2,1,0:T(8,128)S(1)}, u32[]{:S(2)}) copy-start(f32[3,200,768]{2,1,0:T(8,128)S(1)} %get-tuple-element.202.hat_hbm) | copy-start | bytes 5529604
  46.4 19.1 %copy-start = (bf16[2,256,384]{2,1,0:T(8,128)(2,1)S(1)}, bf16[2,256,384]{2,1,0:T(8,128)(2,1)}, u32[]{:S(2)}) copy-start(bf16[2,256,384]{2,1,0:T(8,128)(2,1)} %constant.20.clone.tv_ref) | copy-start | bytes 1179652
  46.4 19.1 %copy-start.1 = (f32[2,6,9216]{2,0,1:T(2,128)S(1)}, f32[2,6,9216]{2,0,1:T(2,128)}, u32[]{:S(2)}) copy-start(f32[2,6,9216]{2,0,1:T(2,128)} %param.22) | copy-start | bytes 1327108
  46.5 19.1 %copy-start.17 = (f32[864,128]{1,0:T(8,128)S(1)}, f32[864,128]{1,0:T(8,128)}, u32[]{:S(2)}) copy-start(f32[864,128]{1,0:T(8,128)} %get-tuple-element.203.their_hbm) | copy-start | bytes 1327108
  67.1 12.9 %collective-permute-start.12 = (f32[872,128]{1,0:T(8,128)S(1)}, f32[872,128]{1,0:T(8,128)S(1)}, u32[]{:S(2)}, u32[]{:S(2)}) collective-permute-start(f32[872,128]{1,0:T(8,128)S(1)} %get-tuple-element.192), channel_id=1, source_target_pairs={{0,96},{16,112},{32,64},{48,80},{64,32},{80,48},{96,0},{112,16},{1... | collective-permute-start | bytes 1339400 | tf_op jit(solution)/shard_map/cond/branch_5_fun/ppermute | solution.py:353
